TPU v7x, 256 devices: a whole 4x4x8 slice. The times are simulated.
256 devices in a mesh: dp: 16 (over y, x), rows: 16 (over z, core).
Axes of the slice: x: 4, y: 4, z: 8, core: 2. Of those that a mesh axis runs over, the one named last changes fastest.
Arguments:
- grad_out: bfloat16 [8192, 4096], P('dp', 'rows'), may hold values from -0.375 to 0.375
- activations: bfloat16 [8192, 4096], P('dp', 'rows'), may hold values from -6 to 6
- error_feedback: float32 [16, 4096, 4096], P('dp', 'rows'), may hold values from -6 to 6
- momentum: bfloat16 [4096, 4096], P('rows'), may hold values from -1.1953125 to 1.1953125
- right_factor: float32 [4096, 128], P('rows'), may hold values from -0.09375 to 0.09375
Outputs:
- new_error: float32 [16, 4096, 4096], P('dp', 'rows')
- new_momentum: bfloat16 [4096, 4096], P('rows')
- new_right: float32 [4096, 128], P('rows')
All inputs are finite; a program needn't handle non-finite values.
Results may differ from a plain program's by a relative error of at most 0.0012.
Values may be sent and summed in bfloat16 or wider, within the bound.
A program may use at most 64 MiB of HBM per device.

v0:
```python
import jax
import jax.numpy as jnp
from jax import lax
from jax.sharding import PartitionSpec as P

PASSES = 2


MOMENTUM_RATE = 0.9
HIGHEST = lax.Precision.HIGHEST


def from_everyone(value, axis):
    copies = jnp.broadcast_to(value, (lax.axis_size(axis), *value.shape))
    return lax.all_to_all(copies, axis, split_axis=0, concat_axis=0, tiled=True)


def joined_along(tiles, dim):
    lengths = list(tiles.shape[1:])
    lengths[dim] *= tiles.shape[0]
    return jnp.moveaxis(tiles, 0, dim).reshape(lengths)


def gathered_copies(value, axis, dim):
    tiles = from_everyone(value, axis)
    return joined_along(tiles, dim)


def of_everyone(value, axis):
    everything = from_everyone(value, axis)
    return jnp.sum(everything, axis=0)


def total_of_pieces(value, axis):
    return lax.all_gather(value, axis).sum(0)


def cut_along(value, dim, count):
    lengths = value.shape
    tiles = value.reshape(*lengths[:dim], count, lengths[dim] // count, *lengths[dim + 1 :])
    return jnp.moveaxis(tiles, dim, 0)


def sent_and_summed(value, axis, dim):
    count = lax.axis_size(axis)
    tiles = lax.all_to_all(cut_along(value, dim, count), axis, 0, 0, tiled=True)
    return jnp.sum(tiles, axis=0)


def per_device(grad_out, activations, error_feedback, momentum, right_factor):
    replicas = lax.axis_size("dp")
    grad_local = lax.dot_general(
        grad_out,
        lax.all_gather(activations, "rows", axis=1, tiled=True),
        (((0,), (0,)), ((), ())),
        preferred_element_type=jnp.float32,
    )
    merged = grad_local + error_feedback[0]
    right_full = gathered_copies(right_factor, "rows", 0)
    left_factor = None
    own_rows = None
    for pass_index in range(PASSES):
        local_term = jnp.dot(
            merged, right_full, precision=HIGHEST, preferred_element_type=jnp.float32
        )
        left_factor = of_everyone(local_term, "dp") / replicas
        gram_local = jnp.dot(
            left_factor.T, left_factor, precision=HIGHEST, preferred_element_type=jnp.float32
        )
        gram_matrix = total_of_pieces(gram_local, "rows")
        cholesky_lower = jnp.linalg.cholesky(gram_matrix)
        left_factor = jax.scipy.linalg.solve_triangular(cholesky_lower, left_factor.T, lower=True).T
        right_term = lax.dot_general(
            merged,
            left_factor,
            (((0,), (0,)), ((), ())),
            precision=HIGHEST,
            preferred_element_type=jnp.float32,
        )
        own_rows = sent_and_summed(right_term, "rows", 0)
        own_rows = of_everyone(own_rows, "dp") / replicas
        right_full = gathered_copies(own_rows, "rows", 0)
    approx = jnp.dot(
        left_factor, right_full.T, precision=HIGHEST, preferred_element_type=jnp.float32
    )
    new_error = (merged - approx)[None]
    new_momentum = (MOMENTUM_RATE * momentum.astype(jnp.float32) + approx).astype(jnp.bfloat16)
    return (new_error, new_momentum, own_rows)


def solution(mesh):
    return jax.shard_map(
        per_device,
        mesh=mesh,
        in_specs=(
            P("dp", "rows"),
            P("dp", "rows"),
            P("dp", "rows", None),
            P("rows", None),
            P("rows", None),
        ),
        out_specs=(P("dp", "rows", None), P("rows", None), P("rows", None)),
        check_vma=False,
    )
```

profile of v0, /device:TPU:1, one launch (start us, length us, event | category | flops | bytes accessed | tf_op | source)
XLA Modules:
  0.0 616.3 jit_solution(16566047498738973250)
XLA Ops:
  7.9 2.4 broadcast_in_dim.25
  10.3 10.0 %all-to-all-start = ((f32[16,256,128]{2,1,0:T(8,128)}), f32[16,256,128]{2,1,0:T(8,128)S(1)}, u32[]{:S(2)}, u32[]{:S(2)}) async-start(f32[16,256,128]{2,1,0:T(8,128)} %broadcast_in_dim.25), calls=%async_computation | async-start | bytes 4194304 | tf_op jit(solution)/shard_map/all_to_all | solution.py:15
  20.4 75.3 %all-gather.6.cloned.1.call-done = bf16[512,4096]{1,0:T(8,128)(2,1)} async-done(((bf16[512,256]{1,0:T(8,128)(2,1)}), bf16[512,4096]{1,0:T(8,128)(2,1)}) %all-gather.6.cloned.1.call-update) | async-done | bytes 4194320 | tf_op jit(solution)/shard_map/all_gather | solution.py:54
  95.7 6.8 %convolution_add_fusion = f32[256,4096]{1,0:T(8,128)} fusion(bf16[512,256]{1,0:T(8,128)(2,1)S(1)} %copy-done, bf16[512,4096]{1,0:T(8,128)(2,1)} %all-gather.6.cloned.1.call-done, f32[1,256,4096]{2,1,0:T(8,128)} %param.10), kind=kOutput, calls=%fused_computation | convolution fusion | flops 1074790400 | bytes 12845056 | tf_op jit(solution)/shard_map/dot_general | solution.py:52
  102.5 5.9 fusion.26
  108.6 34.5 %all_to_all.45 = f32[16,256,128]{2,1,0:T(8,128)S(1)} all-to-all(f32[16,256,128]{2,1,0:T(8,128)S(1)} %broadcast_in_dim.26), channel_id=1, replica_groups=mesh['dp'=16,'rows'=16] {'dp'}, dimensions={0} | all-to-all | bytes 4194304 | tf_op jit(solution)/shard_map/all_to_all | solution.py:15
  144.4 34.3 %all-gather.8.cloned.1.call-done = f32[2048,128]{1,0:T(8,128)} async-done(((f32[128,128]{1,0:T(8,128)}), f32[2048,128]{1,0:T(8,128)}) %all-gather.8.cloned.1.call-update) | async-done | bytes 1048592 | tf_op jit(solution)/shard_map/all_gather | solution.py:35
  178.7 1.3 reduce_sum.73
  180.1 11.7 %cholesky.44 = f32[128,128]{1,0:T(8,128)S(1)} custom-call(f32[128,128]{1,0:T(8,128)S(1)} %fusion.15), custom_call_target="Cholesky" | custom-call | tf_op jit(solution)/shard_map/jit(cholesky)/cholesky | solution.py:71
  193.2 9.8 %custom-call.6 = f32[1,128,128]{1,2,0:T(8,128)S(1)} custom-call(f32[1,128,128]{2,1,0:T(8,128)S(1)} %fusion.10), custom_call_target="InvertDiagBlocksLowerTriangular" | custom-call | tf_op jit(solution)/shard_map/jit(_solve_triangular)/triangular_solve | solution.py:72
  203.3 8.7 %fusion.27 = f32[4096,128]{1,0:T(8,128)S(1)} fusion(f32[256,4096]{1,0:T(8,128)} %convolution_add_fusion, f32[128,256]{1,0:T(8,128)S(1)} %fusion.2), kind=kOutput, calls=%fused_computation.41 | convolution fusion | flops 1610612736 | bytes 6422528 | tf_op jit(solution)/shard_map/dot_general | solution.py:73
  212.0 55.3 %all_to_all.46 = f32[16,256,128]{2,1,0:T(8,128)S(1)} all-to-all(f32[16,256,128]{2,1,0:T(8,128)S(1)} %bitcast.49), channel_id=1, replica_groups=mesh['dp'=16,'rows'=16] {'rows'}, dimensions={0} | all-to-all | bytes 4194304 | tf_op jit(solution)/shard_map/all_to_all | solution.py:46
  267.6 34.7 %all_to_all.47 = f32[16,256,128]{2,1,0:T(8,128)S(1)} all-to-all(f32[16,256,128]{2,1,0:T(8,128)S(1)} %broadcast_in_dim.27), channel_id=1, replica_groups=mesh['dp'=16,'rows'=16] {'dp'}, dimensions={0} | all-to-all | bytes 4194304 | tf_op jit(solution)/shard_map/all_to_all | solution.py:15
  302.6 54.5 %all_to_all.48 = f32[16,256,128]{2,1,0:T(8,128)S(1)} all-to-all(f32[16,256,128]{2,1,0:T(8,128)S(1)} %broadcast_in_dim.28), channel_id=1, replica_groups=mesh['dp'=16,'rows'=16] {'rows'}, dimensions={0} | all-to-all | bytes 4194304 | tf_op jit(solution)/shard_map/all_to_all | solution.py:15
  357.1 3.5 fusion.28
  360.8 31.1 %all_to_all.49 = f32[16,256,128]{2,1,0:T(8,128)S(1)} all-to-all(f32[16,256,128]{2,1,0:T(8,128)S(1)} %broadcast_in_dim.29), channel_id=1, replica_groups=mesh['dp'=16,'rows'=16] {'dp'}, dimensions={0} | all-to-all | bytes 4194304 | tf_op jit(solution)/shard_map/all_to_all | solution.py:15
  393.0 32.6 %all-gather.10.cloned.1.call-done = f32[2048,128]{1,0:T(8,128)} async-done(((f32[128,128]{1,0:T(8,128)}), f32[2048,128]{1,0:T(8,128)}) %all-gather.10.cloned.1.call-update) | async-done | bytes 1048592 | tf_op jit(solution)/shard_map/all_gather | solution.py:35
  427.0 11.7 %cholesky.55 = f32[128,128]{1,0:T(8,128)S(1)} custom-call(f32[128,128]{1,0:T(8,128)S(1)} %fusion.13), custom_call_target="Cholesky" | custom-call | tf_op jit(solution)/shard_map/jit(cholesky)/cholesky | solution.py:71
  440.1 9.8 %custom-call.7 = f32[1,128,128]{1,2,0:T(8,128)S(1)} custom-call(f32[1,128,128]{2,1,0:T(8,128)S(1)} %fusion.11), custom_call_target="InvertDiagBlocksLowerTriangular" | custom-call | tf_op jit(solution)/shard_map/jit(_solve_triangular)/triangular_solve | solution.py:72
  450.2 8.7 %fusion.29 = f32[4096,128]{1,0:T(8,128)S(1)} fusion(f32[256,4096]{1,0:T(8,128)} %convolution_add_fusion, f32[128,256]{1,0:T(8,128)S(1)} %fusion), kind=kOutput, calls=%fused_computation.43 | convolution fusion | flops 1610612736 | bytes 6422528 | tf_op jit(solution)/shard_map/dot_general | solution.py:73
  458.8 55.3 %all_to_all.50 = f32[16,256,128]{2,1,0:T(8,128)S(1)} all-to-all(f32[16,256,128]{2,1,0:T(8,128)S(1)} %bitcast.51), channel_id=1, replica_groups=mesh['dp'=16,'rows'=16] {'rows'}, dimensions={0} | all-to-all | bytes 4194304 | tf_op jit(solution)/shard_map/all_to_all | solution.py:46
  514.4 34.7 %all_to_all.51 = f32[16,256,128]{2,1,0:T(8,128)S(1)} all-to-all(f32[16,256,128]{2,1,0:T(8,128)S(1)} %broadcast_in_dim.30), channel_id=1, replica_groups=mesh['dp'=16,'rows'=16] {'dp'}, dimensions={0} | all-to-all | bytes 4194304 | tf_op jit(solution)/shard_map/all_to_all | solution.py:15
  549.5 54.5 %all_to_all.52 = f32[16,256,128]{2,1,0:T(8,128)S(1)} all-to-all(f32[16,256,128]{2,1,0:T(8,128)S(1)} %broadcast_in_dim.31), channel_id=1, replica_groups=mesh['dp'=16,'rows'=16] {'rows'}, dimensions={0} | all-to-all | bytes 4194304 | tf_op jit(solution)/shard_map/all_to_all | solution.py:15
  604.0 5.8 add_convert_fusion
  (46 shorter events, 9.7 us)
Async XLA Ops:
  7.2 88.5 %copy-start = (bf16[512,256]{1,0:T(8,128)(2,1)S(1)}, bf16[512,256]{1,0:T(8,128)(2,1)}, u32[]{:S(2)}) copy-start(bf16[512,256]{1,0:T(8,128)(2,1)} %param.8) | copy-start | bytes 786436
  7.2 88.5 %all-gather.6.cloned.1.call-start = ((), (), s32[]{:S(2)}) async-start(), calls=%async_computation.9 | async-start | bytes 4456448 | tf_op jit(solution)/shard_map/all_gather | solution.py:54
  10.3 92.1 %all-to-all-start = ((f32[16,256,128]{2,1,0:T(8,128)}), f32[16,256,128]{2,1,0:T(8,128)S(1)}, u32[]{:S(2)}, u32[]{:S(2)}) async-start(f32[16,256,128]{2,1,0:T(8,128)} %broadcast_in_dim.25), calls=%async_computation | async-start | bytes 4194304 | tf_op jit(solution)/shard_map/all_to_all | solution.py:15
  20.3 158.4 %all-gather.8.cloned.1.call-start = ((), (), s32[]{:S(2)}) async-start(), calls=%async_computation.10 | async-start | bytes 1114112 | tf_op jit(solution)/shard_map/all_gather | solution.py:35
  144.2 281.4 %all-gather.10.cloned.1.call-start = ((), (), s32[]{:S(2)}) async-start(), calls=%async_computation.11 | async-start | bytes 1114112 | tf_op jit(solution)/shard_map/all_gather | solution.py:35
  302.6 54.6 %copy-start.1 = (f32[256,4096]{1,0:T(8,128)S(1)}, f32[256,4096]{1,0:T(8,128)}, u32[]{:S(2)}) copy-start(f32[256,4096]{1,0:T(8,128)} %convolution_add_fusion) | copy-start | bytes 12582916
  549.2 54.8 %copy-start.4 = (f32[256,128]{1,0:T(8,128)}, f32[256,128]{1,0:T(8,128)S(1)}, u32[]{:S(2)}) copy-start(f32[256,128]{1,0:T(8,128)S(1)} %broadcast_multiply_fusion) | copy-start | bytes 393220
  549.2 54.8 %copy-start.3 = (bf16[256,4096]{1,0:T(8,128)(2,1)S(1)}, bf16[256,4096]{1,0:T(8,128)(2,1)}, u32[]{:S(2)}) copy-start(bf16[256,4096]{1,0:T(8,128)(2,1)} %param.11) | copy-start | bytes 6291460
  549.5 54.6 %copy-start.2 = (f32[256,4096]{1,0:T(8,128)S(1)}, f32[256,4096]{1,0:T(8,128)}, u32[]{:S(2)}) copy-start(f32[256,4096]{1,0:T(8,128)} %convolution_add_fusion) | copy-start | bytes 12582916
Sparse Core Ops, SparseCore 0:
  9.7 85.8 all-gather.5
  144.3 34.3 all-gather.7
  393.1 32.4 all-gather.9
where the time goes:
time: 617 us; the launch traced here: 616 us
  blocking collectives  355 us (58%)
  waiting for transfers between devices  143 us (23%)
  other arithmetic  49 us (8%)
  matrix products  41.9 us (7%)
  between operations  14 us (2%)
  starting transfers between devices  10.3 us (2%)
    all_to_all x6, blocking collectives, from_everyone(): return lax.all_to_all(copies, axis, split_axis=0, concat_axis=0, tiled=True)  244 us
    all_to_all x2, blocking collectives, sent_and_summed(): tiles = lax.all_to_all(cut_along(value, dim, count), axis, 0, 0, tiled=True)  111 us
    all_gather x1, waiting for transfers between devices, per_device(): lax.all_gather(activations, 'rows', axis=1, tiled=True)  75.3 us
    all_gather x2, waiting for transfers between devices, total_of_pieces(): return lax.all_gather(value, axis).sum(0)  66.9 us
    another operation x6, other arithmetic, per_device(): cholesky_lower = jnp.linalg.cholesky(gram_matrix)  24.8 us
    another operation x4, other arithmetic, per_device(): jax.scipy.linalg.solve_triangular(cholesky_lower, left_factor.T, lower=True)  20.9 us
    dot_general x2, matrix products, per_device(): lax.dot_general(merged, left_factor, (((0,), (0,)), ((), ())), precision=...  17.3 us
  transfers between devices with their start and end apart: 4, of which 3 were waited for; matrix products, arithmetic and copies ran while one was open for 1% of the time, Pallas kernels for 0%

commit v1 on v0

v1 whole, which is shorter than its diff:
```python
import functools

import jax
import jax.numpy as jnp
from jax import lax
from jax.experimental import pallas as pl
from jax.experimental.pallas import tpu as pltpu
from jax.sharding import PartitionSpec as P

MOMENTUM_RATE = 0.9
HIGHEST = lax.Precision.HIGHEST
MESH = pl.DeviceIdType.MESH
F32 = jnp.float32
PANEL = 16


def dot32(a, b, dims=((1,), (0,))):
    return lax.dot_general(
        a, b, (dims, ((), ())), precision=HIGHEST, preferred_element_type=F32
    )


def ring_dist(delta, size):
    return min(delta, size - delta)


def far_first(n_a, n_b, weight):
    pairs = [(a, b) for a in range(n_a) for b in range(n_b) if a or b]
    return sorted(pairs, key=lambda p: -weight(*p))


def cholesky_panels(aug, first, last):
    k = aug.shape[0]

    def panel(p, carry):
        base = pl.multiple_of(p * PANEL, PANEL)
        rows = aug[pl.ds(base, PANEL), :]
        lane = lax.broadcasted_iota(jnp.int32, (PANEL, 2 * k), 1)
        sub = lax.broadcasted_iota(jnp.int32, (PANEL, 1), 0)
        left = rows[:, :k]
        lane_k = lax.broadcasted_iota(jnp.int32, (PANEL, k), 1)
        cols = [
            jnp.sum(jnp.where(lane_k == base + i, left, 0.0), axis=1, keepdims=True)
            for i in range(PANEL)
        ]
        for i in range(PANEL):
            scale = lax.rsqrt(cols[i][i : i + 1, :])
            factor = jnp.where(sub > i, cols[i] * scale, 0.0)
            keep = sub == i
            head = rows[i : i + 1, :] * scale
            rows = jnp.where(keep, head, rows - factor * head)
            for m in range(i + 1, PANEL):
                cols[m] = cols[m] - factor * (cols[m][i : i + 1, :] * scale)
        aug[pl.ds(base, PANEL), :] = rows
        upper = jnp.where(lane_k >= base + PANEL, rows[:, :k], 0.0)
        aug[...] = aug[...] - dot32(upper.T, rows)
        return carry

    lax.fori_loop(first, last, panel, 0)


def body(
    nx, ny, nz, scale,
    grad, act, err, right0,
    merged_out, lhat_out, s_out, sown_out, inv_out,
    act_all, grad_t, err_v, merged, rb, m_tile, m_t,
    xr, yr, xs, ys, xf, yf, top, bottom,
    p_plane, r_plane, f_plane, p_col, r_col, f_col, aug, s_full,
    local_sem, up_send, up_recv, down_send, down_recv, sib_send, sib_recv,
    rb_send, rb_recv, x_send, x_recv, y_send, y_recv, xf_send, xf_recv, yf_send, yf_recv,
    ps_send, ps_recv, pg_send, pg_recv, cs_send, cs_recv, cg_send, cg_recv,
    ag_send, ag_recv, dd_send, dd_recv,
):
    d, j = lax.axis_index("dp"), lax.axis_index("rows")
    y, x = d // nx, d % nx
    z, c = j // 2, j % 2
    tok, cb = act.shape
    rb_rows = grad.shape[1]
    half_rows = rb_rows // 2
    n = nx * ny
    far = nz // 2
    th = tok // 2

    def plane_id(dy, dx):
        return (((y + dy) % ny) * nx + (x + dx) % nx, j)

    def col_id(dz, dc):
        return (d, ((z + dz) % nz) * 2 + (c + dc) % 2)

    plane = far_first(ny, nx, lambda a, b: ring_dist(a, ny) + ring_dist(b, nx))
    column = far_first(nz, 2, lambda a, b: ring_dist(a, nz) + 0.1 * b)

    def remote(src, dst, send, recv, device):
        return pltpu.make_async_remote_copy(
            src_ref=src, dst_ref=dst, send_sem=send, recv_sem=recv,
            device_id=device, device_id_type=MESH,
        )

    load_act = pltpu.make_async_copy(act, act_all.at[0, 0], local_sem.at[0])
    load_act.start()
    load_err = pltpu.make_async_copy(err.at[0], err_v, local_sem.at[1])
    load_err.start()

    barrier = pltpu.get_barrier_semaphore()
    for dy, dx in plane:
        pl.semaphore_signal(barrier, inc=1, device_id=plane_id(dy, dx), device_id_type=MESH)
    for dz, dc in column:
        pl.semaphore_signal(barrier, inc=1, device_id=col_id(dz, dc), device_id_type=MESH)
    grad_t[...] = grad[...].astype(F32).T.astype(jnp.bfloat16)
    load_act.wait()
    pl.semaphore_wait(barrier, len(plane) + len(column))

    def half(slot, h):
        return act_all.at[slot, 0, pl.ds(h * th, th)]

    def up(s, h):
        return remote(half((nz - s + 1) % nz, h), half(nz - s, h), up_send.at[s - 1, h], up_recv.at[s - 1, h], col_id(1, 0))

    def down(s, h):
        return remote(half(s - 1, h), half(s, h), down_send.at[s - 1, h], down_recv.at[s - 1, h], col_id(nz - 1, 0))

    def sibling(slot, h):
        return remote(half(slot, h), act_all.at[slot, 1, pl.ds(h * th, th)], sib_send.at[slot, h], sib_recv.at[slot, h], col_id(0, 1))

    up_list = [(s, h) for s in range(1, far) for h in (0, 1)] + [(far, 0)]
    down_list = [(s, h) for s in range(1, far) for h in (1, 0)] + [(far, 1)]

    for ua, da in zip(up_list[:2], down_list[:2]):
        if ua[0] == 1:
            up(*ua).start()
        if da[0] == 1:
            down(*da).start()
    for h in (0, 1):
        sibling(0, h).start()

    own_block = x * ny + y
    src_z, src_c = own_block // 2, own_block % 2
    rb_up = remote(rb, rb, rb_send.at[0], rb_recv, col_id(1, 0))
    rb_down = remote(rb, rb, rb_send.at[1], rb_recv, col_id(nz - 1, 0))
    rb_sib = remote(rb, rb, rb_send.at[2], rb_recv, col_id(0, 1))

    @pl.when(jnp.logical_and(z == src_z, c == src_c))
    def _():
        own = pltpu.make_async_copy(right0, rb, local_sem.at[2])
        own.start()
        own.wait()
        rb_up.start()
        if far > 1:
            rb_down.start()
        rb_sib.start()

    def relay_rb(s, upward):
        at = (z - s) if upward else (z + s)

        @pl.when(jnp.logical_and((at + nz) % nz == src_z, c == src_c))
        def _():
            rb_up.wait_recv()
            if upward and s < far:
                rb_up.start()
            if not upward and s < far - 1:
                rb_down.start()
            rb_sib.start()

    load_err.wait()
    def block_of(slot, dc):
        return ((z + slot) % nz) * 2 + (c + dc) % 2

    def columns(b):
        return pl.ds(pl.multiple_of(b * cb, cb), cb)

    def x_copy(b, dx):
        return remote(merged.at[pl.ds(0, half_rows), columns(b)], xr.at[b % ny, dx - 1],
                      x_send.at[b], x_recv.at[b % ny, dx - 1], plane_id(0, dx))

    def y_copy(b, dy):
        return remote(merged.at[pl.ds(half_rows, half_rows), columns(b)], yr.at[b // ny, dy - 1],
                      y_send.at[b], y_recv.at[b // ny, dy - 1], plane_id(dy, 0))

    def produce(slot, dc):
        if dc == 1:
            hs = (0, 1)
            for h in hs:
                sibling(slot, h).wait_recv()
        b = block_of(slot, dc)
        cols = columns(b)
        tile = jnp.dot(grad_t[...], act_all[slot, dc], preferred_element_type=F32)
        merged[:, cols] = tile + err_v[:, cols]
        owner_x, owner_y = b // ny, b % ny
        for dx in range(1, nx):
            @pl.when((owner_x - x + nx) % nx == dx)
            def _(dx=dx):
                x_copy(b, dx).start()
        for dy in range(1, ny):
            @pl.when((owner_y - y + ny) % ny == dy)
            def _(dy=dy):
                y_copy(b, dy).start()

    def xf_copy(dy):
        return remote(xs.at[dy - 1], xf.at[dy - 1], xf_send.at[dy - 1], xf_recv.at[dy - 1], plane_id(dy, 0))

    def yf_copy(dx):
        return remote(ys.at[dx - 1], yf.at[dx - 1], yf_send.at[dx - 1], yf_recv.at[dx - 1], plane_id(0, dx))

    def consume(slot, dc):
        b = block_of(slot, dc)
        cols = columns(b)
        owner_x, owner_y = b // ny, b % ny

        @pl.when(owner_x == x)
        def _():
            total = merged[pl.ds(0, half_rows), cols]
            for dx in range(1, nx):
                x_copy(b, dx).wait_recv()
                total = total + xr[b % ny, dx - 1]

            @pl.when(owner_y == y)
            def _():
                top[...] = total
            for dy in range(1, ny):
                @pl.when((owner_y - y + ny) % ny == dy)
                def _(dy=dy):
                    xs[dy - 1] = total
                    xf_copy(dy).start()

        @pl.when(owner_y == y)
        def _():
            total = merged[pl.ds(half_rows, half_rows), cols]
            for dy in range(1, ny):
                y_copy(b, dy).wait_recv()
                total = total + yr[b // ny, dy - 1]

            @pl.when(owner_x == x)
            def _():
                bottom[...] = total
            for dx in range(1, nx):
                @pl.when((owner_x - x + nx) % nx == dx)
                def _(dx=dx):
                    ys[dx - 1] = total
                    yf_copy(dx).start()

    produce(0, 0)
    later = {i: [] for i in range(nz + 3)}
    later[0].append((0, 1))
    for i, ((s, h), (t, g)) in enumerate(zip(up_list, down_list)):
        if s < far and h == 1:
            later[i] += [(nz - s, 0), (s, 0)]
            later[i + 1] += [(nz - s, 1), (s, 1)]
        if s == far:
            later[i] += [(far, 0)]
            later[i + 1] += [(far, 1)]
    done = [(0, 0)]
    steps = len(up_list)
    for i in range(steps + 1):
        if i < steps:
            (s, h), (t, g) = up_list[i], down_list[i]
            up(s, h).wait_recv()
            if s + 1 < far or (s + 1 == far and h == 0):
                up(s + 1, h).start()
            sibling(nz - s, h).start()
            down(t, g).wait_recv()
            if t + 1 < far or (t + 1 == far and g == 1):
                down(t + 1, g).start()
            sibling(t, g).start()
            if s == far or h == 1:
                relay_rb(s, True)
                if s < far:
                    relay_rb(s, False)
        fresh = later[i]
        for slot, dc in fresh:
            produce(slot, dc)
        for slot, dc in done:
            consume(slot, dc)
        done = list(fresh)
    for slot, dc in done:
        consume(slot, dc)

    store_merged = pltpu.make_async_copy(merged, merged_out, local_sem.at[1])
    store_merged.start()

    @pl.when(c != src_c)
    def _():
        rb_sib.wait_recv()

    acc = top[...]
    for dy in range(1, ny):
        xf_copy(dy).wait_recv()
        acc = acc + xf[dy - 1]
    m_tile[pl.ds(0, half_rows), :] = acc * scale
    acc = bottom[...]
    for dx in range(1, nx):
        yf_copy(dx).wait_recv()
        acc = acc + yf[dx - 1]
    m_tile[pl.ds(half_rows, half_rows), :] = acc * scale

    sr = rb_rows // n
    gr = aug.shape[0] // n
    k = aug.shape[0]

    def wait_bytes(ref, sem):
        pltpu.make_async_copy(ref, ref, sem).wait()

    def plane_scatter(stage):
        for i, (dy, dx) in enumerate(plane):
            dev = plane_id(dy, dx)
            remote(p_plane.at[stage, dev[0]], r_plane.at[stage, i], ps_send.at[stage], ps_recv.at[stage], dev).start()

    def plane_gather(stage):
        wait_bytes(r_plane.at[stage], ps_recv.at[stage])
        total = p_plane[stage, d]
        for i in range(len(plane)):
            total = total + r_plane[stage, i]
        f_plane[stage, d] = total
        for dy, dx in plane:
            remote(f_plane.at[stage, d], f_plane.at[stage, d], pg_send.at[stage], pg_recv.at[stage], plane_id(dy, dx)).start()

    def plane_finish(stage):
        wait_bytes(r_plane.at[stage], pg_recv.at[stage])
        return f_plane[stage].reshape(rb_rows, k)

    def col_scatter(stage):
        for i, (dz, dc) in enumerate(column):
            dev = col_id(dz, dc)
            remote(p_col.at[stage, dev[1]], r_col.at[stage, i], cs_send.at[stage], cs_recv.at[stage], dev).start()

    def col_gather(stage):
        wait_bytes(r_col.at[stage], cs_recv.at[stage])
        total = p_col[stage, j]
        for i in range(len(column)):
            total = total + r_col[stage, i]
        f_col[stage, j] = total
        for dz, dc in column:
            remote(f_col.at[stage, j], f_col.at[stage, j], cg_send.at[stage], cg_recv.at[stage], col_id(dz, dc)).start()

    def col_finish(stage):
        wait_bytes(r_col.at[stage], cg_recv.at[stage])
        both = f_col[stage]
        return both[:, :sr].reshape(cb, k), both[:, sr:].reshape(k, k)

    def set_aug(gram):
        row = lax.broadcasted_iota(jnp.int32, (k, k), 0)
        col = lax.broadcasted_iota(jnp.int32, (k, k), 1)
        aug[:, :k] = gram
        aug[:, k:] = jnp.where(row == col, 1.0, 0.0).astype(F32)

    panels = k // PANEL

    p_plane[0] = dot32(m_tile[...], rb[...]).reshape(n, sr, k)
    plane_scatter(0)
    m_t[...] = m_tile[...].T
    plane_gather(0)
    left = plane_finish(0)
    p_col[0, :, :sr] = dot32(m_t[...], left).reshape(n, sr, k)
    p_col[0, :, sr:] = dot32(left, left, ((0,), (0,))).reshape(n, gr, k)
    col_scatter(0)
    col_gather(0)
    s_one, gram_one = col_finish(0)
    p_plane[1] = dot32(m_tile[...], s_one).reshape(n, sr, k)
    plane_scatter(1)
    set_aug(gram_one)
    cholesky_panels(aug, 0, panels // 2)
    plane_gather(1)
    cholesky_panels(aug, panels // 2, panels)
    left = dot32(plane_finish(1), aug[:, k:], ((1,), (1,)))
    p_col[1, :, :sr] = dot32(m_t[...], left).reshape(n, sr, k)
    p_col[1, :, sr:] = dot32(left, left, ((0,), (0,))).reshape(n, gr, k)
    col_scatter(1)
    col_gather(1)
    _, gram_two = col_finish(1)

    hc = cb // 2
    own_half = f_col[1, pl.ds(c * (n // 2), n // 2), :sr, :].reshape(hc, k)
    s_full[x, y, pl.ds(pl.multiple_of(c * hc, hc), hc), :] = own_half
    q = hc // 2
    q0 = pl.ds(pl.multiple_of(c * hc, hc), q)
    q1 = pl.ds(pl.multiple_of(c * hc + q, q), q)

    def ag1x(dx):
        ref = s_full.at[x, y, q0]
        return remote(ref, ref, ag_send.at[0, dx - 1], ag_recv.at[0, dx - 1], plane_id(0, dx))

    def ag1y(dy):
        ref = s_full.at[x, y, q1]
        return remote(ref, ref, ag_send.at[1, dy - 1], ag_recv.at[1, dy - 1], plane_id(dy, 0))

    def ag2x(dy):
        ref = s_full.at[:, y, q0]
        return remote(ref, ref, ag_send.at[2, dy - 1], ag_recv.at[2, dy - 1], plane_id(dy, 0))

    def ag2y(dx):
        ref = s_full.at[x, :, q1]
        return remote(ref, ref, ag_send.at[3, dx - 1], ag_recv.at[3, dx - 1], plane_id(0, dx))

    def d2d(i, where):
        ref = s_full.at[where]
        return remote(ref, ref, dd_send.at[i], dd_recv.at[i], col_id(0, 1))

    for dx in range(1, nx):
        ag1x(dx).start()
    for dy in range(1, ny):
        ag1y(dy).start()
    set_aug(gram_two)
    cholesky_panels(aug, 0, panels // 2)
    for dx in range(1, nx):
        ag1x(dx).wait_recv()
    for dy in range(1, ny):
        ag2x(dy).start()
    for dy in range(1, ny):
        ag1y(dy).wait_recv()
    for dx in range(1, nx):
        ag2y(dx).start()
    cholesky_panels(aug, panels // 2, panels)
    inverse = aug[:, k:]
    inv_out[...] = inverse
    lhat_out[...] = dot32(dot32(left, inverse, ((1,), (1,))), inverse)

    for dy in range(1, ny):
        ag2x(dy).wait_recv()
    for dx in range(1, nx):
        ag2y(dx).wait_recv()
    share = d2d(0, (slice(None), slice(None), pl.ds(pl.multiple_of(c * hc, hc), hc)))
    share.start()
    share.wait_recv()
    store_s = pltpu.make_async_copy(s_full, s_out, local_sem.at[0])
    store_s.start()
    sown_out[...] = s_full[j // ny, j % ny]

    for s, h in up_list:
        up(s, h).wait_send()
    for s, h in down_list:
        down(s, h).wait_send()
    for slot in range(nz):
        for h in (0, 1):
            sibling(slot, h).wait_send()
    is_src_core = c == src_c
    away = (z - src_z + nz) % nz

    @pl.when(jnp.logical_and(is_src_core, away < far))
    def _():
        rb_up.wait_send()
    if far > 1:
        @pl.when(jnp.logical_and(is_src_core, jnp.logical_or(away == 0, away > far + 1)))
        def _():
            rb_down.wait_send()

    @pl.when(is_src_core)
    def _():
        rb_sib.wait_send()
    for b in range(n):
        if nx > 1:
            @pl.when(b // ny != x)
            def _(b=b):
                x_copy(b, 1).wait_send()
        if ny > 1:
            @pl.when(b % ny != y)
            def _(b=b):
                y_copy(b, 1).wait_send()
    for dy in range(1, ny):
        xf_copy(dy).wait_send()
        ag1y(dy).wait_send()
        ag2x(dy).wait_send()
    for dx in range(1, nx):
        yf_copy(dx).wait_send()
        ag1x(dx).wait_send()
        ag2y(dx).wait_send()
    for stage in (0, 1):
        wait_bytes(r_plane.at[stage], ps_send.at[stage])
        wait_bytes(r_plane.at[stage], pg_send.at[stage])
        wait_bytes(r_col.at[stage], cs_send.at[stage])
        wait_bytes(r_col.at[stage], cg_send.at[stage])
    share.wait_send()
    store_merged.wait()
    store_s.wait()


def finish_body(merged, lhat, s, momentum, sown, inverse, error, new_momentum, right):
    approx = dot32(lhat[...], s[...], ((1,), (1,)))
    error[0] = merged[...] - approx
    new_momentum[...] = (MOMENTUM_RATE * momentum[...].astype(F32) + approx).astype(jnp.bfloat16)

    @pl.when(pl.program_id(0) == 0)
    def _():
        right[...] = dot32(sown[...], inverse[...], ((1,), (1,)))


def per_device(nx, ny, nz, grad_out, activations, error_feedback, momentum, right_factor):
    n = nx * ny
    tok, cb = activations.shape
    rows = grad_out.shape[1]
    total = error_feedback.shape[2]
    k = right_factor.shape[1]
    sr, gr, hr = rows // n, k // n, rows // 2
    far = nz // 2
    vmem, dma = pltpu.VMEM, pltpu.SemaphoreType.DMA
    scratch = [
        vmem((nz, 2, tok, cb), jnp.bfloat16),
        vmem((rows, tok), jnp.bfloat16),
        vmem((rows, total), F32),
        vmem((rows, total), F32),
        vmem((cb, k), F32),
        vmem((rows, cb), F32),
        vmem((cb, rows), F32),
        vmem((ny, max(nx - 1, 1), hr, cb), F32),
        vmem((nx, max(ny - 1, 1), hr, cb), F32),
        vmem((max(ny - 1, 1), hr, cb), F32),
        vmem((max(nx - 1, 1), hr, cb), F32),
        vmem((max(ny - 1, 1), hr, cb), F32),
        vmem((max(nx - 1, 1), hr, cb), F32),
        vmem((hr, cb), F32),
        vmem((hr, cb), F32),
        vmem((2, n, sr, k), F32),
        vmem((2, n - 1, sr, k), F32),
        vmem((2, n, sr, k), F32),
        vmem((2, n, sr + gr, k), F32),
        vmem((2, n - 1, sr + gr, k), F32),
        vmem((2, n, sr + gr, k), F32),
        vmem((k, 2 * k), F32),
        vmem((nx, ny, cb, k), F32),
        dma((3,)),
        dma((far, 2)), dma((far, 2)), dma((far, 2)), dma((far, 2)),
        dma((nz, 2)), dma((nz, 2)),
        dma((3,)), dma,
        dma((n,)), dma((ny, max(nx - 1, 1))),
        dma((n,)), dma((nx, max(ny - 1, 1))),
        dma((max(ny - 1, 1),)), dma((max(ny - 1, 1),)),
        dma((max(nx - 1, 1),)), dma((max(nx - 1, 1),)),
        dma((2,)), dma((2,)), dma((2,)), dma((2,)),
        dma((2,)), dma((2,)), dma((2,)), dma((2,)),
        dma((4, max(nx, ny))), dma((4, max(nx, ny))),
        dma((1,)), dma((1,)),
    ]
    any_space = pl.BlockSpec(memory_space=pl.ANY)
    in_vmem = pl.BlockSpec(memory_space=pltpu.VMEM)
    merged, lhat, s, sown, inverse = pl.pallas_call(
        functools.partial(body, nx, ny, nz, 1.0 / n),
        out_shape=(
            jax.ShapeDtypeStruct((rows, total), F32),
            jax.ShapeDtypeStruct((rows, k), F32),
            jax.ShapeDtypeStruct((nx, ny, cb, k), F32),
            jax.ShapeDtypeStruct((cb, k), F32),
            jax.ShapeDtypeStruct((k, k), F32),
        ),
        in_specs=[in_vmem, any_space, any_space, any_space],
        out_specs=(any_space, in_vmem, any_space, in_vmem, in_vmem),
        scratch_shapes=scratch,
        compiler_params=pltpu.CompilerParams(
            collective_id=0, has_side_effects=True, vmem_limit_bytes=48 << 20
        ),
        name="compress",
    )(grad_out, activations, error_feedback, right_factor)
    s = s.reshape(n * cb, k)
    wide = min(512, total)
    return pl.pallas_call(
        finish_body,
        grid=(total // wide,),
        out_shape=(
            jax.ShapeDtypeStruct((1, rows, total), F32),
            jax.ShapeDtypeStruct((rows, total), jnp.bfloat16),
            jax.ShapeDtypeStruct((cb, k), F32),
        ),
        in_specs=[
            pl.BlockSpec((rows, wide), lambda i: (0, i)),
            pl.BlockSpec((rows, k), lambda i: (0, 0)),
            pl.BlockSpec((wide, k), lambda i: (i, 0)),
            pl.BlockSpec((rows, wide), lambda i: (0, i)),
            pl.BlockSpec((cb, k), lambda i: (0, 0)),
            pl.BlockSpec((k, k), lambda i: (0, 0)),
        ],
        out_specs=(
            pl.BlockSpec((1, rows, wide), lambda i: (0, 0, i)),
            pl.BlockSpec((rows, wide), lambda i: (0, i)),
            pl.BlockSpec((cb, k), lambda i: (0, 0)),
        ),
        name="finish",
    )(merged, lhat, s, momentum, sown, inverse)


def build(mesh, nx, ny, nz):
    return jax.shard_map(
        functools.partial(per_device, nx, ny, nz),
        mesh=mesh,
        in_specs=(
            P("dp", "rows"),
            P("dp", "rows"),
            P("dp", "rows", None),
            P("rows", None),
            P("rows", None),
        ),
        out_specs=(P("dp", "rows", None), P("rows", None), P("rows", None)),
        check_vma=False,
    )


def solution(mesh):
    return build(mesh, 4, 4, 8)
```

time: 617 us -> 167 us (0.27)
  blocking collectives: 355 us -> 0 us
  Pallas kernels: 0 us -> 160 us
  waiting for transfers between devices: 143 us -> 0 us
  other arithmetic: 49 us -> 0 us
  matrix products: 41.9 us -> 0 us
  between operations: 14 us -> 0.82 us
  starting transfers between devices: 10.3 us -> 0 us
    all_to_all x8 -> x0, blocking collectives: 355 us -> none  [the longest x6 244 us: from_everyone(): return lax.all_to_all(copies, axis, split_axis=0, concat_axis=0, tiled=True)]
    pallas_call x0 -> x2, Pallas kernels: none -> 160 us  [the longest x1 149 us: per_device(): pl.pallas_call(functools.partial(body, nx, ny, nz, 1.0 / n), out_shape=(j...]
    all_gather x3 -> x0, waiting for transfers between devices: 142 us -> none  [the longest x1 75.3 us: per_device(): lax.all_gather(activations, 'rows', axis=1, tiled=True)]
    another operation x10 -> x0, other arithmetic: 45.7 us -> none  [the longest x6 24.8 us: per_device(): cholesky_lower = jnp.linalg.cholesky(gram_matrix)]
    dot_general x8 -> x0, matrix products: 41.3 us -> none  [the longest x2 17.3 us: per_device(): lax.dot_general(merged, left_factor, (((0,), (0,)), ((), ())), precision=...]
    all_to_all x1 -> x0, starting transfers between devices: 9.97 us -> none  [from_everyone(): return lax.all_to_all(copies, axis, split_axis=0, concat_axis=0, tiled=True)]
  transfers between devices with their start and end apart: 4 -> 0, of which waited for: 3 -> 0; matrix products, arithmetic and copies ran while one was open for 1% -> 0% of each run, Pallas kernels for 0% -> 0%
where the time goes in v1:
time: 167 us; the launch traced here: 166 us
  Pallas kernels  160 us (96%)
  local copies, waits for them, and re-layouts  6.03 us (4%)
    pallas_call x1, Pallas kernels, per_device(): pl.pallas_call(functools.partial(body, nx, ny, nz, 1.0 / n), out_shape=(j...  149 us
    pallas_call x1, Pallas kernels, per_device(): pl.pallas_call(finish_body, grid=(total // wide,), out_shape=(jax.ShapeDt...  10.2 us
    unnamed x14, local copies, waits for them, and re-layouts  6.03 us

profile of v1, /device:TPU:1, one launch (start us, length us, event | category | flops | bytes accessed | tf_op | source)
XLA Modules:
  0.0 166.5 jit_solution(2164523541068417116)
XLA Ops:
  0.6 0.0 copy-start.1
  0.6 0.9 copy-done.1
  1.6 0.0 copy-start.2
  1.6 0.9 copy-done.2
  2.5 0.0 copy-start.5
  2.5 0.9 copy-done.5
  3.4 149.5 %compress.1 = (f32[256,4096]{1,0:T(8,128)}, f32[256,128]{1,0:T(8,128)S(1)}, f32[4,4,256,128]{3,2,1,0:T(8,128)S(1)}, f32[256,128]{1,0:T(8,128)S(1)}, f32[128,128]{1,0:T(8,128)S(1)}) custom-call(bf16[512,256]{1,0:T(8,128)(2,1)S(1)} %copy-done.1, bf16[512,256]{1,0:T(8,128)(2,1)S(1)} %copy-done.2, f32[1,256,4096]{2,1,0:T(8,128)} %err.1, f32[256,128]{1,0:T(8,128)S(1)} %copy-done.5), custom_call_target="tpu_custom_call" | custom-call | tf_op jit(solution)/shard_map/compress/pallas_call | solution.py:533
  152.9 0.0 copy-start
  152.9 1.3 copy-done
  154.2 0.0 copy-start.3
  154.2 0.6 copy-done.3
  154.9 0.0 copy-start.4
  154.9 0.6 copy-done.4
  155.5 0.0 copy-start.6
  155.5 0.6 copy-done.6
  156.2 10.2 %finish.1 = (f32[1,256,4096]{2,1,0:T(8,128)}, bf16[256,4096]{1,0:T(8,128)(2,1)}, f32[256,128]{1,0:T(8,128)}) custom-call(f32[256,4096]{1,0:T(8,128)} %get-tuple-element.8.merged, f32[256,128]{1,0:T(8,128)} %copy-done.3, f32[4096,128]{1,0:T(8,128)} %bitcast.1, bf16[256,4096]{1,0:T(8,128)(2,1)} %momentum.1, f32[256,128]{1,0:T(8,128)} %copy-done.4, ...), custom_call_target="tpu_custom_call" | custom-call | tf_op jit(solution)/shard_map/finish/pallas_call | solution.py:552
Async XLA Ops:
  0.6 1.0 copy-start.1
  1.6 0.9 copy-start.2
  2.5 0.9 copy-start.5
  152.9 1.3 copy-start
  154.2 0.7 copy-start.3
  154.9 0.6 copy-start.4
  155.5 0.6 copy-start.6

commit v2 on v1

--- a/solution.py
+++ b/solution.py
@@ -12,6 +12,9 @@
 MESH = pl.DeviceIdType.MESH
 F32 = jnp.float32
 PANEL = 16
+SCALE_ROWS = 16
+LAG = 3
+VMEM_LIMIT = 33_554_432
 
 
 def dot32(a, b, dims=((1,), (0,))):
@@ -27,6 +30,24 @@
 def far_first(n_a, n_b, weight):
     pairs = [(a, b) for a in range(n_a) for b in range(n_b) if a or b]
     return sorted(pairs, key=lambda p: -weight(*p))
+
+
+def encode(v):
+    peak = jnp.max(jnp.max(jnp.abs(v), axis=0, keepdims=True), axis=1, keepdims=True)
+    peak = jnp.maximum(peak, 1e-30).astype(jnp.bfloat16).astype(F32)
+    t = v * (1024.0 / peak)
+    t4 = (t * t) * (t * t)
+    t12 = t4 * t4 * t4
+    code = jnp.where(v < 0, -t12, t12).astype(jnp.bfloat16)
+    return code, jnp.broadcast_to(peak, (SCALE_ROWS, v.shape[1])).astype(jnp.bfloat16)
+
+
+def decode(code, peak):
+    y = code.astype(F32)
+    size = jnp.abs(y)
+    r = jnp.exp2(jnp.log2(jnp.maximum(size, 1e-37)) * (1.0 / 12.0) - 10.0)
+    r = jnp.where(size > 1e-37, r, 0.0) * peak[:1].astype(F32)
+    return jnp.where(y < 0, -r, r)
 
 
 def cholesky_panels(aug, first, last):
@@ -61,11 +82,11 @@
 
 def body(
     nx, ny, nz, scale,
-    grad, act, err, right0,
-    merged_out, lhat_out, s_out, sown_out, inv_out,
-    act_all, grad_t, err_v, merged, rb, m_tile, m_t,
-    xr, yr, xs, ys, xf, yf, top, bottom,
-    p_plane, r_plane, f_plane, p_col, r_col, f_col, aug, s_full,
+    grad, act, err, right0, momentum,
+    merged, lhat_out, s_full, sown_out, inv_out, momentum_out,
+    grad_v, act_all, grad_t, err_v, rb, m_tile, m_t,
+    xt, yt, xr, yr, xs, ys, xf, yf, top, bottom,
+    p_plane, r_plane, f_plane, p_col, r_col, f_col, aug,
     local_sem, up_send, up_recv, down_send, down_recv, sib_send, sib_recv,
     rb_send, rb_recv, x_send, x_recv, y_send, y_recv, xf_send, xf_recv, yf_send, yf_recv,
     ps_send, ps_recv, pg_send, pg_recv, cs_send, cs_recv, cg_send, cg_recv,
@@ -98,17 +119,20 @@
 
     load_act = pltpu.make_async_copy(act, act_all.at[0, 0], local_sem.at[0])
     load_act.start()
+    load_grad = pltpu.make_async_copy(grad, grad_v, local_sem.at[3])
+    load_grad.start()
     load_err = pltpu.make_async_copy(err.at[0], err_v, local_sem.at[1])
     load_err.start()
 
     barrier = pltpu.get_barrier_semaphore()
-    for dy, dx in plane:
-        pl.semaphore_signal(barrier, inc=1, device_id=plane_id(dy, dx), device_id_type=MESH)
-    for dz, dc in column:
-        pl.semaphore_signal(barrier, inc=1, device_id=col_id(dz, dc), device_id_type=MESH)
-    grad_t[...] = grad[...].astype(F32).T.astype(jnp.bfloat16)
+    near = [plane_id(dy, 0) for dy in range(1, ny)] + [plane_id(0, dx) for dx in range(1, nx)]
+    near += [col_id(dz, 0) for dz in sorted({1, nz - 1})] + [col_id(0, 1)]
+    for device in near:
+        pl.semaphore_signal(barrier, inc=1, device_id=device, device_id_type=MESH)
     load_act.wait()
-    pl.semaphore_wait(barrier, len(plane) + len(column))
+    pl.semaphore_wait(barrier, len(near))
+
+    pending = []
 
     def half(slot, h):
         return act_all.at[slot, 0, pl.ds(h * th, th)]
@@ -125,6 +149,16 @@
     up_list = [(s, h) for s in range(1, far) for h in (0, 1)] + [(far, 0)]
     down_list = [(s, h) for s in range(1, far) for h in (1, 0)] + [(far, 1)]
 
+    def gather_sent():
+        for s, h in up_list:
+            up(s, h).wait_send()
+        for s, h in down_list:
+            down(s, h).wait_send()
+        for slot in range(nz):
+            for h in (0, 1):
+                sibling(slot, h).wait_send()
+
+    pending.append(gather_sent)
     for ua, da in zip(up_list[:2], down_list[:2]):
         if ua[0] == 1:
             up(*ua).start()
@@ -149,6 +183,23 @@
             rb_down.start()
         rb_sib.start()
 
+    def rb_sent():
+        away = (z - src_z + nz) % nz
+
+        @pl.when(jnp.logical_and(c == src_c, away < far))
+        def _():
+            rb_up.wait_send()
+        if far > 1:
+            @pl.when(jnp.logical_and(c == src_c, jnp.logical_or(away == 0, away > far + 1)))
+            def _():
+                rb_down.wait_send()
+
+        @pl.when(c == src_c)
+        def _():
+            rb_sib.wait_send()
+
+    pending.append(rb_sent)
+
     def relay_rb(s, upward):
         at = (z - s) if upward else (z + s)
 
@@ -161,39 +212,55 @@
                 rb_down.start()
             rb_sib.start()
 
+    load_grad.wait()
+    grad_t[...] = grad_v[...].astype(F32).T.astype(jnp.bfloat16)
     load_err.wait()
+    load_momentum = pltpu.make_async_copy(momentum, momentum_out, local_sem.at[1])
+    load_momentum.start()
+    pending.append(load_momentum.wait)
     def block_of(slot, dc):
         return ((z + slot) % nz) * 2 + (c + dc) % 2
 
     def columns(b):
         return pl.ds(pl.multiple_of(b * cb, cb), cb)
 
-    def x_copy(b, dx):
-        return remote(merged.at[pl.ds(0, half_rows), columns(b)], xr.at[b % ny, dx - 1],
-                      x_send.at[b], x_recv.at[b % ny, dx - 1], plane_id(0, dx))
-
-    def y_copy(b, dy):
-        return remote(merged.at[pl.ds(half_rows, half_rows), columns(b)], yr.at[b // ny, dy - 1],
-                      y_send.at[b], y_recv.at[b // ny, dy - 1], plane_id(dy, 0))
+    def x_copy(b, dx, slot=0):
+        return remote(xt.at[slot], xr.at[b % ny, dx - 1],
+                      x_send.at[slot], x_recv.at[b % ny, dx - 1], plane_id(0, dx))
+
+    def y_copy(b, dy, slot=0):
+        return remote(yt.at[slot], yr.at[b // ny, dy - 1],
+                      y_send.at[slot], y_recv.at[b // ny, dy - 1], plane_id(dy, 0))
+
+    def put(ref, index, v):
+        code, peak = encode(v)
+        ref[index, :half_rows] = code
+        ref[index, half_rows:] = peak
+
+    def get(ref, *index):
+        message = ref[index]
+        return decode(message[:half_rows], message[half_rows:])
 
     def produce(slot, dc):
         if dc == 1:
-            hs = (0, 1)
-            for h in hs:
+            for h in (0, 1):
                 sibling(slot, h).wait_recv()
         b = block_of(slot, dc)
         cols = columns(b)
-        tile = jnp.dot(grad_t[...], act_all[slot, dc], preferred_element_type=F32)
-        merged[:, cols] = tile + err_v[:, cols]
+        tile = jnp.dot(grad_t[...], act_all[slot, dc], preferred_element_type=F32) + err_v[:, cols]
+        merged[:, cols] = tile
         owner_x, owner_y = b // ny, b % ny
-        for dx in range(1, nx):
-            @pl.when((owner_x - x + nx) % nx == dx)
-            def _(dx=dx):
-                x_copy(b, dx).start()
-        for dy in range(1, ny):
-            @pl.when((owner_y - y + ny) % ny == dy)
-            def _(dy=dy):
-                y_copy(b, dy).start()
+        at = 2 * slot + dc
+        if nx > 1:
+            @pl.when(owner_x != x)
+            def _():
+                put(xt, at, tile[:half_rows])
+                x_copy(b, (owner_x - x + nx) % nx, at).start()
+        if ny > 1:
+            @pl.when(owner_y != y)
+            def _():
+                put(yt, at, tile[half_rows:])
+                y_copy(b, (owner_y - y + ny) % ny, at).start()
 
     def xf_copy(dy):
         return remote(xs.at[dy - 1], xf.at[dy - 1], xf_send.at[dy - 1], xf_recv.at[dy - 1], plane_id(dy, 0))
@@ -211,71 +278,86 @@
             total = merged[pl.ds(0, half_rows), cols]
             for dx in range(1, nx):
                 x_copy(b, dx).wait_recv()
-                total = total + xr[b % ny, dx - 1]
+                total = total + get(xr, b % ny, dx - 1)
 
             @pl.when(owner_y == y)
             def _():
                 top[...] = total
-            for dy in range(1, ny):
-                @pl.when((owner_y - y + ny) % ny == dy)
-                def _(dy=dy):
-                    xs[dy - 1] = total
-                    xf_copy(dy).start()
+
+            @pl.when(owner_y != y)
+            def _():
+                dy = (owner_y - y + ny) % ny
+                put(xs, dy - 1, total)
+                xf_copy(dy).start()
 
         @pl.when(owner_y == y)
         def _():
             total = merged[pl.ds(half_rows, half_rows), cols]
             for dy in range(1, ny):
                 y_copy(b, dy).wait_recv()
-                total = total + yr[b // ny, dy - 1]
+                total = total + get(yr, b // ny, dy - 1)
 
             @pl.when(owner_x == x)
             def _():
                 bottom[...] = total
-            for dx in range(1, nx):
-                @pl.when((owner_x - x + nx) % nx == dx)
-                def _(dx=dx):
-                    ys[dx - 1] = total
-                    yf_copy(dx).start()
-
+
+            @pl.when(owner_x != x)
+            def _():
+                dx = (owner_x - x + nx) % nx
+                put(ys, dx - 1, total)
+                yf_copy(dx).start()
+
+    def tiles_sent():
+        for slot in range(nz):
+            for dc in (0, 1):
+                b, at = block_of(slot, dc), 2 * slot + dc
+
+                @pl.when(b // ny != x)
+                def _(b=b, at=at):
+                    x_copy(b, 1, at).wait_send()
+
+                @pl.when(b % ny != y)
+                def _(b=b, at=at):
+                    y_copy(b, 1, at).wait_send()
+        for dy in range(1, ny):
+            xf_copy(dy).wait_send()
+        for dx in range(1, nx):
+            yf_copy(dx).wait_send()
+
+    pending.append(tiles_sent)
     produce(0, 0)
     later = {i: [] for i in range(nz + 3)}
     later[0].append((0, 1))
     for i, ((s, h), (t, g)) in enumerate(zip(up_list, down_list)):
         if s < far and h == 1:
-            later[i] += [(nz - s, 0), (s, 0)]
-            later[i + 1] += [(nz - s, 1), (s, 1)]
+            later[i] += [(nz - s, 0), (s, 0), (nz - s, 1), (s, 1)]
         if s == far:
-            later[i] += [(far, 0)]
-            later[i + 1] += [(far, 1)]
-    done = [(0, 0)]
+            later[i] += [(far, 0), (far, 1)]
+    waiting = [[(0, 0)]]
     steps = len(up_list)
-    for i in range(steps + 1):
-        if i < steps:
-            (s, h), (t, g) = up_list[i], down_list[i]
-            up(s, h).wait_recv()
-            if s + 1 < far or (s + 1 == far and h == 0):
-                up(s + 1, h).start()
-            sibling(nz - s, h).start()
-            down(t, g).wait_recv()
-            if t + 1 < far or (t + 1 == far and g == 1):
-                down(t + 1, g).start()
-            sibling(t, g).start()
-            if s == far or h == 1:
-                relay_rb(s, True)
-                if s < far:
-                    relay_rb(s, False)
-        fresh = later[i]
-        for slot, dc in fresh:
+    for i in range(steps):
+        (s, h), (t, g) = up_list[i], down_list[i]
+        up(s, h).wait_recv()
+        if s + 1 < far or (s + 1 == far and h == 0):
+            up(s + 1, h).start()
+        sibling(nz - s, h).start()
+        down(t, g).wait_recv()
+        if t + 1 < far or (t + 1 == far and g == 1):
+            down(t + 1, g).start()
+        sibling(t, g).start()
+        if s == far or h == 1:
+            relay_rb(s, True)
+            if s < far:
+                relay_rb(s, False)
+        for slot, dc in later[i]:
             produce(slot, dc)
-        for slot, dc in done:
+        waiting.append(later[i])
+        if len(waiting) > LAG:
+            for slot, dc in waiting.pop(0):
+                consume(slot, dc)
+    for group in waiting:
+        for slot, dc in group:
             consume(slot, dc)
-        done = list(fresh)
-    for slot, dc in done:
-        consume(slot, dc)
-
-    store_merged = pltpu.make_async_copy(merged, merged_out, local_sem.at[1])
-    store_merged.start()
 
     @pl.when(c != src_c)
     def _():
@@ -284,12 +366,12 @@
     acc = top[...]
     for dy in range(1, ny):
         xf_copy(dy).wait_recv()
-        acc = acc + xf[dy - 1]
+        acc = acc + get(xf, dy - 1)
     m_tile[pl.ds(0, half_rows), :] = acc * scale
     acc = bottom[...]
     for dx in range(1, nx):
         yf_copy(dx).wait_recv()
-        acc = acc + yf[dx - 1]
+        acc = acc + get(yf, dx - 1)
     m_tile[pl.ds(half_rows, half_rows), :] = acc * scale
 
     sr = rb_rows // n
@@ -300,6 +382,8 @@
         pltpu.make_async_copy(ref, ref, sem).wait()
 
     def plane_scatter(stage):
+        pending.append(lambda: wait_bytes(r_plane.at[stage], ps_send.at[stage]))
+        pending.append(lambda: wait_bytes(r_plane.at[stage], pg_send.at[stage]))
         for i, (dy, dx) in enumerate(plane):
             dev = plane_id(dy, dx)
             remote(p_plane.at[stage, dev[0]], r_plane.at[stage, i], ps_send.at[stage], ps_recv.at[stage], dev).start()
@@ -318,6 +402,8 @@
         return f_plane[stage].reshape(rb_rows, k)
 
     def col_scatter(stage):
+        pending.append(lambda: wait_bytes(r_col.at[stage], cs_send.at[stage]))
+        pending.append(lambda: wait_bytes(r_col.at[stage], cg_send.at[stage]))
         for i, (dz, dc) in enumerate(column):
             dev = col_id(dz, dc)
             remote(p_col.at[stage, dev[1]], r_col.at[stage, i], cs_send.at[stage], cs_recv.at[stage], dev).start()
@@ -394,6 +480,15 @@
         ref = s_full.at[where]
         return remote(ref, ref, dd_send.at[i], dd_recv.at[i], col_id(0, 1))
 
+    def right_sent():
+        for dy in range(1, ny):
+            ag1y(dy).wait_send()
+            ag2x(dy).wait_send()
+        for dx in range(1, nx):
+            ag1x(dx).wait_send()
+            ag2y(dx).wait_send()
+
+    pending.append(right_sent)
     for dx in range(1, nx):
         ag1x(dx).start()
     for dy in range(1, ny):
@@ -420,66 +515,43 @@
     share = d2d(0, (slice(None), slice(None), pl.ds(pl.multiple_of(c * hc, hc), hc)))
     share.start()
     share.wait_recv()
-    store_s = pltpu.make_async_copy(s_full, s_out, local_sem.at[0])
-    store_s.start()
     sown_out[...] = s_full[j // ny, j % ny]
 
-    for s, h in up_list:
-        up(s, h).wait_send()
-    for s, h in down_list:
-        down(s, h).wait_send()
-    for slot in range(nz):
-        for h in (0, 1):
-            sibling(slot, h).wait_send()
-    is_src_core = c == src_c
-    away = (z - src_z + nz) % nz
-
-    @pl.when(jnp.logical_and(is_src_core, away < far))
-    def _():
-        rb_up.wait_send()
-    if far > 1:
-        @pl.when(jnp.logical_and(is_src_core, jnp.logical_or(away == 0, away > far + 1)))
-        def _():
-            rb_down.wait_send()
-
-    @pl.when(is_src_core)
-    def _():
-        rb_sib.wait_send()
-    for b in range(n):
-        if nx > 1:
-            @pl.when(b // ny != x)
-            def _(b=b):
-                x_copy(b, 1).wait_send()
-        if ny > 1:
-            @pl.when(b % ny != y)
-            def _(b=b):
-                y_copy(b, 1).wait_send()
-    for dy in range(1, ny):
-        xf_copy(dy).wait_send()
-        ag1y(dy).wait_send()
-        ag2x(dy).wait_send()
-    for dx in range(1, nx):
-        yf_copy(dx).wait_send()
-        ag1x(dx).wait_send()
-        ag2y(dx).wait_send()
-    for stage in (0, 1):
-        wait_bytes(r_plane.at[stage], ps_send.at[stage])
-        wait_bytes(r_plane.at[stage], pg_send.at[stage])
-        wait_bytes(r_col.at[stage], cs_send.at[stage])
-        wait_bytes(r_col.at[stage], cg_send.at[stage])
+    for wait in pending:
+        wait()
     share.wait_send()
-    store_merged.wait()
-    store_s.wait()
-
-
-def finish_body(merged, lhat, s, momentum, sown, inverse, error, new_momentum, right):
-    approx = dot32(lhat[...], s[...], ((1,), (1,)))
-    error[0] = merged[...] - approx
-    new_momentum[...] = (MOMENTUM_RATE * momentum[...].astype(F32) + approx).astype(jnp.bfloat16)
-
-    @pl.when(pl.program_id(0) == 0)
-    def _():
-        right[...] = dot32(sown[...], inverse[...], ((1,), (1,)))
+
+
+def split(v):
+    high = v.astype(jnp.bfloat16)
+    return high, (v - high.astype(F32)).astype(jnp.bfloat16)
+
+
+def finish_body(wide, merged, lhat, s, momentum, sown, inverse, error, new_momentum, right, e_buf, m_buf, sem):
+    total = merged.shape[1]
+    l_high, l_low = split(lhat[...])
+    l_all = jnp.concatenate([l_high, l_high, l_low], axis=1)
+
+    def copies(i):
+        cols = pl.ds(i * wide, wide)
+        return (
+            pltpu.make_async_copy(e_buf.at[i], error.at[0, :, cols], sem.at[i, 0]),
+            pltpu.make_async_copy(m_buf.at[i], new_momentum.at[:, cols], sem.at[i, 1]),
+        )
+
+    for i in range(total // wide):
+        cols = pl.ds(i * wide, wide)
+        s_high, s_low = split(s[cols, :])
+        s_all = jnp.concatenate([s_high, s_low, s_high], axis=1)
+        approx = lax.dot_general(l_all, s_all, (((1,), (1,)), ((), ())), preferred_element_type=F32)
+        e_buf[i] = merged[:, cols] - approx
+        m_buf[i] = (MOMENTUM_RATE * momentum[:, cols].astype(F32) + approx).astype(jnp.bfloat16)
+        for copy in copies(i):
+            copy.start()
+    right[...] = dot32(sown[...], inverse[...], ((1,), (1,)))
+    for i in range(total // wide):
+        for copy in copies(i):
+            copy.wait()
 
 
 def per_device(nx, ny, nz, grad_out, activations, error_feedback, momentum, right_factor):
@@ -492,19 +564,21 @@
     far = nz // 2
     vmem, dma = pltpu.VMEM, pltpu.SemaphoreType.DMA
     scratch = [
+        vmem((tok, rows), jnp.bfloat16),
         vmem((nz, 2, tok, cb), jnp.bfloat16),
         vmem((rows, tok), jnp.bfloat16),
-        vmem((rows, total), F32),
         vmem((rows, total), F32),
         vmem((cb, k), F32),
         vmem((rows, cb), F32),
         vmem((cb, rows), F32),
-        vmem((ny, max(nx - 1, 1), hr, cb), F32),
-        vmem((nx, max(ny - 1, 1), hr, cb), F32),
-        vmem((max(ny - 1, 1), hr, cb), F32),
-        vmem((max(nx - 1, 1), hr, cb), F32),
-        vmem((max(ny - 1, 1), hr, cb), F32),
-        vmem((max(nx - 1, 1), hr, cb), F32),
+        vmem((n, hr + SCALE_ROWS, cb), jnp.bfloat16),
+        vmem((n, hr + SCALE_ROWS, cb), jnp.bfloat16),
+        vmem((ny, max(nx - 1, 1), hr + SCALE_ROWS, cb), jnp.bfloat16),
+        vmem((nx, max(ny - 1, 1), hr + SCALE_ROWS, cb), jnp.bfloat16),
+        vmem((max(ny - 1, 1), hr + SCALE_ROWS, cb), jnp.bfloat16),
+        vmem((max(nx - 1, 1), hr + SCALE_ROWS, cb), jnp.bfloat16),
+        vmem((max(ny - 1, 1), hr + SCALE_ROWS, cb), jnp.bfloat16),
+        vmem((max(nx - 1, 1), hr + SCALE_ROWS, cb), jnp.bfloat16),
         vmem((hr, cb), F32),
         vmem((hr, cb), F32),
         vmem((2, n, sr, k), F32),
@@ -514,8 +588,7 @@
         vmem((2, n - 1, sr + gr, k), F32),
         vmem((2, n, sr + gr, k), F32),
         vmem((k, 2 * k), F32),
-        vmem((nx, ny, cb, k), F32),
-        dma((3,)),
+        dma((4,)),
         dma((far, 2)), dma((far, 2)), dma((far, 2)), dma((far, 2)),
         dma((nz, 2)), dma((nz, 2)),
         dma((3,)), dma,
@@ -530,7 +603,7 @@
     ]
     any_space = pl.BlockSpec(memory_space=pl.ANY)
     in_vmem = pl.BlockSpec(memory_space=pltpu.VMEM)
-    merged, lhat, s, sown, inverse = pl.pallas_call(
+    merged, lhat, s, sown, inverse, momentum = pl.pallas_call(
         functools.partial(body, nx, ny, nz, 1.0 / n),
         out_shape=(
             jax.ShapeDtypeStruct((rows, total), F32),
@@ -538,38 +611,33 @@
             jax.ShapeDtypeStruct((nx, ny, cb, k), F32),
             jax.ShapeDtypeStruct((cb, k), F32),
             jax.ShapeDtypeStruct((k, k), F32),
+            jax.ShapeDtypeStruct((rows, total), momentum.dtype),
         ),
-        in_specs=[in_vmem, any_space, any_space, any_space],
-        out_specs=(any_space, in_vmem, any_space, in_vmem, in_vmem),
+        in_specs=[any_space] * 5,
+        out_specs=(in_vmem,) * 6,
         scratch_shapes=scratch,
         compiler_params=pltpu.CompilerParams(
-            collective_id=0, has_side_effects=True, vmem_limit_bytes=48 << 20
+            collective_id=0, has_side_effects=True, vmem_limit_bytes=VMEM_LIMIT
         ),
         name="compress",
-    )(grad_out, activations, error_feedback, right_factor)
+    )(*[pltpu.with_memory_space_constraint(v, pltpu.HBM) for v in (grad_out, activations, error_feedback, right_factor, momentum)])
     s = s.reshape(n * cb, k)
     wide = min(512, total)
     return pl.pallas_call(
-        finish_body,
-        grid=(total // wide,),
+        functools.partial(finish_body, wide),
         out_shape=(
             jax.ShapeDtypeStruct((1, rows, total), F32),
             jax.ShapeDtypeStruct((rows, total), jnp.bfloat16),
             jax.ShapeDtypeStruct((cb, k), F32),
         ),
-        in_specs=[
-            pl.BlockSpec((rows, wide), lambda i: (0, i)),
-            pl.BlockSpec((rows, k), lambda i: (0, 0)),
-            pl.BlockSpec((wide, k), lambda i: (i, 0)),
-            pl.BlockSpec((rows, wide), lambda i: (0, i)),
-            pl.BlockSpec((cb, k), lambda i: (0, 0)),
-            pl.BlockSpec((k, k), lambda i: (0, 0)),
+        in_specs=[in_vmem] * 6,
+        out_specs=(any_space, any_space, in_vmem),
+        scratch_shapes=[
+            vmem((total // wide, rows, wide), F32),
+            vmem((total // wide, rows, wide), jnp.bfloat16),
+            dma((total // wide, 2)),
         ],
-        out_specs=(
-            pl.BlockSpec((1, rows, wide), lambda i: (0, 0, i)),
-            pl.BlockSpec((rows, wide), lambda i: (0, i)),
-            pl.BlockSpec((cb, k), lambda i: (0, 0)),
-        ),
+        compiler_params=pltpu.CompilerParams(vmem_limit_bytes=20 << 20),
         name="finish",
     )(merged, lhat, s, momentum, sown, inverse)
 

time: 167 us -> 119 us (0.71)
  Pallas kernels: 160 us -> 118 us
  local copies, waits for them, and re-layouts: 6.03 us -> 0 us
    pallas_call x1, Pallas kernels: 149 us -> 114 us  [per_device(): pl.pallas_call(functools.partial(body, nx, ny, nz, 1.0 / n), out_shape=(j...]
    pallas_call x1, Pallas kernels: 10.2 us -> 3.84 us  [per_device(): pl.pallas_call(functools.partial(finish_body, wide), out_shape=(jax.Shape...]
    unnamed x14 -> x0, local copies, waits for them, and re-layouts: 6.03 us -> none
where the time goes in v2:
time: 119 us
  Pallas kernels  118 us (99%)
    pallas_call x1, Pallas kernels, per_device(): pl.pallas_call(functools.partial(body, nx, ny, nz, 1.0 / n), out_shape=(j...  114 us
    pallas_call x1, Pallas kernels, per_device(): pl.pallas_call(functools.partial(finish_body, wide), out_shape=(jax.Shape...  3.84 us

profile of v2, /device:TPU:1, one launch (start us, length us, event | category | flops | bytes accessed | tf_op | source)
XLA Modules:
  0.0 118.9 jit_solution(13223320638218070147)
XLA Ops:
  0.6 114.2 %compress.1 = (f32[256,4096]{1,0:T(8,128)S(1)}, f32[256,128]{1,0:T(8,128)S(1)}, f32[4,4,256,128]{3,2,1,0:T(8,128)S(1)}, f32[256,128]{1,0:T(8,128)S(1)}, f32[128,...) custom-call(bf16[512,256]{1,0:T(8,128)(2,1)} %grad.1, bf16[512,256]{1,0:T(8,128)(2,1)} %act.1, f32[1,256,4096]{2,1,0:T(8,128)} %err.1, ...), custom_call_target="tpu_custom_call" | custom-call | tf_op jit(solution)/shard_map/compress/pallas_call | solution.py:606
  114.9 3.8 %finish.1 = (f32[1,256,4096]{2,1,0:T(8,128)}, bf16[256,4096]{1,0:T(8,128)(2,1)}, f32[256,128]{1,0:T(8,128)}) custom-call(f32[256,4096]{1,0:T(8,128)S(1)} %get-tuple-element.9.merged, f32[256,128]{1,0:T(8,128)S(1)} %get-tuple-element.10.lhat, f32[4096,128]{1,0:T(8,128)S(1)} %bitcast.1, bf16[256,4096]{1,0:T(8,128)(2,1)S(1)} %get-tuple-element.12.momentum, ...), custom_call_target="tpu_custom_call" | custom-call | tf_op jit(solution)/shard_map/finish/pallas_call | solution.py:626

commit v3 on v2

--- a/solution.py
+++ b/solution.py
@@ -13,7 +13,8 @@
 F32 = jnp.float32
 PANEL = 16
 SCALE_ROWS = 16
-LAG = 3
+LAG = 5
+PARTS = 4
 VMEM_LIMIT = 33_554_432
 
 
@@ -35,19 +36,35 @@
 def encode(v):
     peak = jnp.max(jnp.max(jnp.abs(v), axis=0, keepdims=True), axis=1, keepdims=True)
     peak = jnp.maximum(peak, 1e-30).astype(jnp.bfloat16).astype(F32)
-    t = v * (1024.0 / peak)
+    t = v * (128.0 / peak)
     t4 = (t * t) * (t * t)
-    t12 = t4 * t4 * t4
-    code = jnp.where(v < 0, -t12, t12).astype(jnp.bfloat16)
+    t8 = t4 * t4
+    t16 = t8 * t8
+    code = jnp.where(v < 0, -t16, t16).astype(jnp.bfloat16)
     return code, jnp.broadcast_to(peak, (SCALE_ROWS, v.shape[1])).astype(jnp.bfloat16)
 
 
 def decode(code, peak):
     y = code.astype(F32)
     size = jnp.abs(y)
-    r = jnp.exp2(jnp.log2(jnp.maximum(size, 1e-37)) * (1.0 / 12.0) - 10.0)
+    r = jnp.exp2(jnp.log2(jnp.maximum(size, 1e-37)) * (1.0 / 16.0) - 7.0)
     r = jnp.where(size > 1e-37, r, 0.0) * peak[:1].astype(F32)
     return jnp.where(y < 0, -r, r)
+
+
+def split(v):
+    high = v.astype(jnp.bfloat16)
+    return high, (v - high.astype(F32)).astype(jnp.bfloat16)
+
+
+def dot_split(a, b):
+    a_high, a_low = split(a)
+    b_high, b_low = split(b)
+    return jnp.dot(
+        jnp.concatenate([a_high, a_high, a_low], axis=1),
+        jnp.concatenate([b_high, b_low, b_high], axis=0),
+        preferred_element_type=F32,
+    )
 
 
 def cholesky_panels(aug, first, last):
@@ -84,12 +101,12 @@
     nx, ny, nz, scale,
     grad, act, err, right0, momentum,
     merged, lhat_out, s_full, sown_out, inv_out, momentum_out,
-    grad_v, act_all, grad_t, err_v, rb, m_tile, m_t,
+    grad_v, act_all, grad_t, err_v, r_all, m_tile, m_t,
     xt, yt, xr, yr, xs, ys, xf, yf, top, bottom,
-    p_plane, r_plane, f_plane, p_col, r_col, f_col, aug,
+    p_plane, r_plane, f_plane, p_col, r_col, f_col, p_gram, r_gram, f_gram, aug,
     local_sem, up_send, up_recv, down_send, down_recv, sib_send, sib_recv,
-    rb_send, rb_recv, x_send, x_recv, y_send, y_recv, xf_send, xf_recv, yf_send, yf_recv,
-    ps_send, ps_recv, pg_send, pg_recv, cs_send, cs_recv, cg_send, cg_recv,
+    rs_send, rs_recv, x_send, x_recv, y_send, y_recv, xf_send, xf_recv, yf_send, yf_recv,
+    ps_send, ps_recv, pg_send, pg_recv, cs_send, cs_recv, cg_send, cg_recv, gs_send, gs_recv, gg_send, gg_recv,
     ag_send, ag_recv, dd_send, dd_recv,
 ):
     d, j = lax.axis_index("dp"), lax.axis_index("rows")
@@ -100,7 +117,7 @@
     half_rows = rb_rows // 2
     n = nx * ny
     far = nz // 2
-    th = tok // 2
+    th = tok // PARTS
 
     def plane_id(dy, dx):
         return (((y + dy) % ny) * nx + (x + dx) % nx, j)
@@ -126,13 +143,97 @@
 
     barrier = pltpu.get_barrier_semaphore()
     near = [plane_id(dy, 0) for dy in range(1, ny)] + [plane_id(0, dx) for dx in range(1, nx)]
-    near += [col_id(dz, 0) for dz in sorted({1, nz - 1})] + [col_id(0, 1)]
+    near += [col_id(dz, 0) for dz in range(1, nz)] + [col_id(0, 1)]
     for device in near:
         pl.semaphore_signal(barrier, inc=1, device_id=device, device_id_type=MESH)
+    sr = rb_rows // n
+    gr = aug.shape[0] // n
+    k = aug.shape[0]
+    load_right = pltpu.make_async_copy(right0.at[pl.ds(pl.multiple_of(d * sr, sr), sr)], r_all.at[x, y, c, z], local_sem.at[2])
+    load_right.start()
     load_act.wait()
+    load_right.wait()
     pl.semaphore_wait(barrier, len(near))
 
     pending = []
+
+    def wait_bytes(ref, sem):
+        pltpu.make_async_copy(ref, ref, sem).wait()
+
+    far_z = sorted(range(1, nz), key=lambda dz: -ring_dist(dz, nz))
+
+    class Everywhere:
+        def __init__(self, buf, which):
+            self.buf, self.which = buf, which
+            half = nz // 2
+            self.q = (pl.ds(0, half), pl.ds(half, nz - half))
+            pending.append(self.sent)
+
+        def column_start(self):
+            ref = self.buf.at[x, y, c, z]
+            for dz in far_z:
+                remote(ref, ref, rs_send.at[self.which], rs_recv.at[self.which], col_id(dz, 0)).start()
+
+        def column_wait(self):
+            wait_bytes(self.buf.at[x, y, c, pl.ds(0, nz - 1)], rs_recv.at[self.which])
+
+        def move(self, step, delta):
+            q = self.q[step % 2]
+            at = (x, y) if step < 2 else ((slice(None), y) if step == 2 else (x, slice(None)))
+            ref = self.buf.at[at[0], at[1], c, q]
+            along_x = step in (0, 3)
+            return remote(ref, ref, ag_send.at[self.which, step, delta - 1], ag_recv.at[self.which, step, delta - 1],
+                          plane_id(0, delta) if along_x else plane_id(delta, 0))
+
+        def share(self, i):
+            if i < ny:
+                ref = self.buf.at[:, (y - i + ny) % ny, c, self.q[0]]
+            else:
+                ref = self.buf.at[(x - (i - ny) + nx) % nx, :, c, self.q[1]]
+            return remote(ref, ref, dd_send.at[self.which, i], dd_recv.at[self.which, i], col_id(0, 1))
+
+        def first(self):
+            for dx in range(1, nx):
+                self.move(0, dx).start()
+            for dy in range(1, ny):
+                self.move(1, dy).start()
+
+        def second(self):
+            for dx in range(1, nx):
+                self.move(0, dx).wait_recv()
+            for dy in range(1, ny):
+                self.move(2, dy).start()
+            for dy in range(1, ny):
+                self.move(1, dy).wait_recv()
+            for dx in range(1, nx):
+                self.move(3, dx).start()
+            self.share(0).start()
+            self.share(ny).start()
+
+        def third(self):
+            for i in range(1, max(nx, ny)):
+                if i < ny:
+                    self.move(2, i).wait_recv()
+                    self.share(i).start()
+                if i < nx:
+                    self.move(3, i).wait_recv()
+                    self.share(ny + i).start()
+
+        def last(self):
+            for i in range(nx + ny):
+                self.share(i).wait_recv()
+
+        def sent(self):
+            wait_bytes(self.buf.at[x, y, c, pl.ds(0, nz - 1)], rs_send.at[self.which])
+            for step in range(4):
+                for delta in range(1, nx if step in (0, 3) else ny):
+                    self.move(step, delta).wait_send()
+            for i in range(nx + ny):
+                self.share(i).wait_send()
+
+    right_in = Everywhere(r_all, 0)
+    right_out = Everywhere(s_full, 1)
+    right_in.column_start()
 
     def half(slot, h):
         return act_all.at[slot, 0, pl.ds(h * th, th)]
@@ -146,8 +247,9 @@
     def sibling(slot, h):
         return remote(half(slot, h), act_all.at[slot, 1, pl.ds(h * th, th)], sib_send.at[slot, h], sib_recv.at[slot, h], col_id(0, 1))
 
-    up_list = [(s, h) for s in range(1, far) for h in (0, 1)] + [(far, 0)]
-    down_list = [(s, h) for s in range(1, far) for h in (1, 0)] + [(far, 1)]
+    mid = PARTS // 2
+    up_list = [(s, h) for s in range(1, far) for h in range(PARTS)] + [(far, h) for h in range(mid)]
+    down_list = [(s, PARTS - 1 - h) for s, h in up_list]
 
     def gather_sent():
         for s, h in up_list:
@@ -155,62 +257,15 @@
         for s, h in down_list:
             down(s, h).wait_send()
         for slot in range(nz):
-            for h in (0, 1):
+            for h in range(PARTS):
                 sibling(slot, h).wait_send()
 
     pending.append(gather_sent)
-    for ua, da in zip(up_list[:2], down_list[:2]):
-        if ua[0] == 1:
-            up(*ua).start()
-        if da[0] == 1:
-            down(*da).start()
-    for h in (0, 1):
+    for ua, da in zip(up_list[:PARTS], down_list[:PARTS]):
+        up(*ua).start()
+        down(*da).start()
+    for h in range(PARTS):
         sibling(0, h).start()
-
-    own_block = x * ny + y
-    src_z, src_c = own_block // 2, own_block % 2
-    rb_up = remote(rb, rb, rb_send.at[0], rb_recv, col_id(1, 0))
-    rb_down = remote(rb, rb, rb_send.at[1], rb_recv, col_id(nz - 1, 0))
-    rb_sib = remote(rb, rb, rb_send.at[2], rb_recv, col_id(0, 1))
-
-    @pl.when(jnp.logical_and(z == src_z, c == src_c))
-    def _():
-        own = pltpu.make_async_copy(right0, rb, local_sem.at[2])
-        own.start()
-        own.wait()
-        rb_up.start()
-        if far > 1:
-            rb_down.start()
-        rb_sib.start()
-
-    def rb_sent():
-        away = (z - src_z + nz) % nz
-
-        @pl.when(jnp.logical_and(c == src_c, away < far))
-        def _():
-            rb_up.wait_send()
-        if far > 1:
-            @pl.when(jnp.logical_and(c == src_c, jnp.logical_or(away == 0, away > far + 1)))
-            def _():
-                rb_down.wait_send()
-
-        @pl.when(c == src_c)
-        def _():
-            rb_sib.wait_send()
-
-    pending.append(rb_sent)
-
-    def relay_rb(s, upward):
-        at = (z - s) if upward else (z + s)
-
-        @pl.when(jnp.logical_and((at + nz) % nz == src_z, c == src_c))
-        def _():
-            rb_up.wait_recv()
-            if upward and s < far:
-                rb_up.start()
-            if not upward and s < far - 1:
-                rb_down.start()
-            rb_sib.start()
 
     load_grad.wait()
     grad_t[...] = grad_v[...].astype(F32).T.astype(jnp.bfloat16)
@@ -243,7 +298,7 @@
 
     def produce(slot, dc):
         if dc == 1:
-            for h in (0, 1):
+            for h in range(PARTS):
                 sibling(slot, h).wait_recv()
         b = block_of(slot, dc)
         cols = columns(b)
@@ -324,44 +379,79 @@
         for dx in range(1, nx):
             yf_copy(dx).wait_send()
 
+    def multiply(pairs):
+        total = jnp.zeros((rb_rows, k), F32)
+        for slot, dc in pairs:
+            b = block_of(slot, dc)
+            strips = [r_all[i, h, b % 2, b // 2] for h in range(ny) for i in range(nx)]
+            total = total + dot_split(merged[:, columns(b)], jnp.concatenate(strips, axis=0))
+        return total
+
+    def plane_scatter(stage):
+        pending.append(lambda: wait_bytes(r_plane.at[stage], ps_send.at[stage]))
+        pending.append(lambda: wait_bytes(r_plane.at[stage], pg_send.at[stage]))
+        for i, (dy, dx) in enumerate(plane):
+            dev = plane_id(dy, dx)
+            remote(p_plane.at[stage, dev[0]], r_plane.at[stage, i], ps_send.at[stage], ps_recv.at[stage], dev).start()
+
+    def plane_gather(stage):
+        wait_bytes(r_plane.at[stage], ps_recv.at[stage])
+        total = p_plane[stage, d]
+        for i in range(len(plane)):
+            total = total + r_plane[stage, i]
+        f_plane[stage, d] = total
+        for dy, dx in plane:
+            remote(f_plane.at[stage, d], f_plane.at[stage, d], pg_send.at[stage], pg_recv.at[stage], plane_id(dy, dx)).start()
+
+    def plane_finish(stage):
+        wait_bytes(r_plane.at[stage], pg_recv.at[stage])
+        return f_plane[stage].reshape(rb_rows, k)
+
     pending.append(tiles_sent)
     produce(0, 0)
-    later = {i: [] for i in range(nz + 3)}
+    later = [[] for _ in range(len(up_list) + 1)]
     later[0].append((0, 1))
-    for i, ((s, h), (t, g)) in enumerate(zip(up_list, down_list)):
-        if s < far and h == 1:
-            later[i] += [(nz - s, 0), (s, 0), (nz - s, 1), (s, 1)]
-        if s == far:
-            later[i] += [(far, 0), (far, 1)]
+    for i, (s, h) in enumerate(up_list):
+        if s < far and h == PARTS - 1:
+            later[i] += [(nz - s, 0), (s, 0)]
+            later[i + 1] += [(nz - s, 1), (s, 1)]
+    later[len(up_list) - 1] += [(far, 0), (far, 1)]
     waiting = [[(0, 0)]]
     steps = len(up_list)
-    for i in range(steps):
-        (s, h), (t, g) = up_list[i], down_list[i]
+    multiplied = []
+    for i, ((s, h), (t, g)) in enumerate(zip(up_list, down_list)):
         up(s, h).wait_recv()
-        if s + 1 < far or (s + 1 == far and h == 0):
+        if s + 1 < far or (s + 1 == far and h < mid):
             up(s + 1, h).start()
         sibling(nz - s, h).start()
         down(t, g).wait_recv()
-        if t + 1 < far or (t + 1 == far and g == 1):
+        if t + 1 < far or (t + 1 == far and g >= mid):
             down(t + 1, g).start()
         sibling(t, g).start()
-        if s == far or h == 1:
-            relay_rb(s, True)
-            if s < far:
-                relay_rb(s, False)
+        if i == min(2, steps - 1):
+            right_in.column_wait()
+            right_in.first()
+        if i == min(6, steps - 1):
+            right_in.second()
+        if i == min(11, steps - 1):
+            right_in.third()
         for slot, dc in later[i]:
             produce(slot, dc)
         waiting.append(later[i])
         if len(waiting) > LAG:
             for slot, dc in waiting.pop(0):
                 consume(slot, dc)
+        if i == max(steps - 2, min(11, steps - 1)):
+            right_in.last()
+            multiplied = [(0, 0)] + [pair for group in later[: i + 1] for pair in group]
+            left_sum = multiply(multiplied)
+    rest = [pair for group in later for pair in group if pair not in multiplied]
+    p_plane[0] = ((left_sum + multiply(rest)) * scale).reshape(n, sr, k)
+    plane_scatter(0)
     for group in waiting:
         for slot, dc in group:
             consume(slot, dc)
-
-    @pl.when(c != src_c)
-    def _():
-        rb_sib.wait_recv()
+    plane_gather(0)
 
     acc = top[...]
     for dy in range(1, ny):
@@ -374,53 +464,48 @@
         acc = acc + get(yf, dx - 1)
     m_tile[pl.ds(half_rows, half_rows), :] = acc * scale
 
-    sr = rb_rows // n
-    gr = aug.shape[0] // n
-    k = aug.shape[0]
-
-    def wait_bytes(ref, sem):
-        pltpu.make_async_copy(ref, ref, sem).wait()
-
-    def plane_scatter(stage):
-        pending.append(lambda: wait_bytes(r_plane.at[stage], ps_send.at[stage]))
-        pending.append(lambda: wait_bytes(r_plane.at[stage], pg_send.at[stage]))
-        for i, (dy, dx) in enumerate(plane):
-            dev = plane_id(dy, dx)
-            remote(p_plane.at[stage, dev[0]], r_plane.at[stage, i], ps_send.at[stage], ps_recv.at[stage], dev).start()
-
-    def plane_gather(stage):
-        wait_bytes(r_plane.at[stage], ps_recv.at[stage])
-        total = p_plane[stage, d]
-        for i in range(len(plane)):
-            total = total + r_plane[stage, i]
-        f_plane[stage, d] = total
-        for dy, dx in plane:
-            remote(f_plane.at[stage, d], f_plane.at[stage, d], pg_send.at[stage], pg_recv.at[stage], plane_id(dy, dx)).start()
-
-    def plane_finish(stage):
-        wait_bytes(r_plane.at[stage], pg_recv.at[stage])
-        return f_plane[stage].reshape(rb_rows, k)
-
-    def col_scatter(stage):
-        pending.append(lambda: wait_bytes(r_col.at[stage], cs_send.at[stage]))
-        pending.append(lambda: wait_bytes(r_col.at[stage], cg_send.at[stage]))
+    factor_col = (p_col, r_col, f_col, cs_send, cs_recv, cg_send, cg_recv)
+    gram_col = (p_gram, r_gram, f_gram, gs_send, gs_recv, gg_send, gg_recv)
+
+    def col_scatter(stage, what, both=True):
+        part, got, full, s_send, s_recv, g_send, g_recv = what
+        pending.append(lambda: wait_bytes(got.at[stage], s_send.at[stage]))
+        if both:
+            pending.append(lambda: wait_bytes(got.at[stage], g_send.at[stage]))
         for i, (dz, dc) in enumerate(column):
             dev = col_id(dz, dc)
-            remote(p_col.at[stage, dev[1]], r_col.at[stage, i], cs_send.at[stage], cs_recv.at[stage], dev).start()
-
-    def col_gather(stage):
-        wait_bytes(r_col.at[stage], cs_recv.at[stage])
-        total = p_col[stage, j]
+            remote(part.at[stage, dev[1]], got.at[stage, i], s_send.at[stage], s_recv.at[stage], dev).start()
+
+    def col_total(stage, what):
+        part, got, full, s_send, s_recv, g_send, g_recv = what
+        wait_bytes(got.at[stage], s_recv.at[stage])
+        total = part[stage, j]
         for i in range(len(column)):
-            total = total + r_col[stage, i]
-        f_col[stage, j] = total
+            total = total + got[stage, i]
+        return total
+
+    def col_gather(stage, what):
+        part, got, full, s_send, s_recv, g_send, g_recv = what
+        full[stage, j] = col_total(stage, what)
         for dz, dc in column:
-            remote(f_col.at[stage, j], f_col.at[stage, j], cg_send.at[stage], cg_recv.at[stage], col_id(dz, dc)).start()
-
-    def col_finish(stage):
-        wait_bytes(r_col.at[stage], cg_recv.at[stage])
-        both = f_col[stage]
-        return both[:, :sr].reshape(cb, k), both[:, sr:].reshape(k, k)
+            remote(full.at[stage, j], full.at[stage, j], g_send.at[stage], g_recv.at[stage], col_id(dz, dc)).start()
+
+    def col_finish(stage, what):
+        part, got, full, s_send, s_recv, g_send, g_recv = what
+        wait_bytes(got.at[stage], g_recv.at[stage])
+        return full[stage].reshape(-1, k)
+
+    def right_of(stage, left):
+        p_col[stage] = dot32(m_t[...], left).reshape(n, sr, k)
+        col_scatter(stage, factor_col, stage == 0)
+        p_gram[stage] = dot32(left, left, ((0,), (0,))).reshape(n, gr, k)
+        col_scatter(stage, gram_col)
+        if stage == 0:
+            col_gather(stage, factor_col)
+        else:
+            s_full[x, y, c, z] = col_total(stage, factor_col)
+            right_out.column_start()
+        col_gather(stage, gram_col)
 
     def set_aug(gram):
         row = lax.broadcasted_iota(jnp.int32, (k, k), 0)
@@ -430,101 +515,43 @@
 
     panels = k // PANEL
 
-    p_plane[0] = dot32(m_tile[...], rb[...]).reshape(n, sr, k)
-    plane_scatter(0)
     m_t[...] = m_tile[...].T
-    plane_gather(0)
     left = plane_finish(0)
-    p_col[0, :, :sr] = dot32(m_t[...], left).reshape(n, sr, k)
-    p_col[0, :, sr:] = dot32(left, left, ((0,), (0,))).reshape(n, gr, k)
-    col_scatter(0)
-    col_gather(0)
-    s_one, gram_one = col_finish(0)
+    right_of(0, left)
+    s_one = col_finish(0, factor_col)
     p_plane[1] = dot32(m_tile[...], s_one).reshape(n, sr, k)
     plane_scatter(1)
-    set_aug(gram_one)
+    set_aug(col_finish(0, gram_col))
     cholesky_panels(aug, 0, panels // 2)
     plane_gather(1)
     cholesky_panels(aug, panels // 2, panels)
     left = dot32(plane_finish(1), aug[:, k:], ((1,), (1,)))
-    p_col[1, :, :sr] = dot32(m_t[...], left).reshape(n, sr, k)
-    p_col[1, :, sr:] = dot32(left, left, ((0,), (0,))).reshape(n, gr, k)
-    col_scatter(1)
-    col_gather(1)
-    _, gram_two = col_finish(1)
-
-    hc = cb // 2
-    own_half = f_col[1, pl.ds(c * (n // 2), n // 2), :sr, :].reshape(hc, k)
-    s_full[x, y, pl.ds(pl.multiple_of(c * hc, hc), hc), :] = own_half
-    q = hc // 2
-    q0 = pl.ds(pl.multiple_of(c * hc, hc), q)
-    q1 = pl.ds(pl.multiple_of(c * hc + q, q), q)
-
-    def ag1x(dx):
-        ref = s_full.at[x, y, q0]
-        return remote(ref, ref, ag_send.at[0, dx - 1], ag_recv.at[0, dx - 1], plane_id(0, dx))
-
-    def ag1y(dy):
-        ref = s_full.at[x, y, q1]
-        return remote(ref, ref, ag_send.at[1, dy - 1], ag_recv.at[1, dy - 1], plane_id(dy, 0))
-
-    def ag2x(dy):
-        ref = s_full.at[:, y, q0]
-        return remote(ref, ref, ag_send.at[2, dy - 1], ag_recv.at[2, dy - 1], plane_id(dy, 0))
-
-    def ag2y(dx):
-        ref = s_full.at[x, :, q1]
-        return remote(ref, ref, ag_send.at[3, dx - 1], ag_recv.at[3, dx - 1], plane_id(0, dx))
-
-    def d2d(i, where):
-        ref = s_full.at[where]
-        return remote(ref, ref, dd_send.at[i], dd_recv.at[i], col_id(0, 1))
-
-    def right_sent():
-        for dy in range(1, ny):
-            ag1y(dy).wait_send()
-            ag2x(dy).wait_send()
-        for dx in range(1, nx):
-            ag1x(dx).wait_send()
-            ag2y(dx).wait_send()
-
-    pending.append(right_sent)
-    for dx in range(1, nx):
-        ag1x(dx).start()
-    for dy in range(1, ny):
-        ag1y(dy).start()
-    set_aug(gram_two)
+    right_of(1, left)
+
+    right_out.column_wait()
+    right_out.first()
+    set_aug(col_finish(1, gram_col))
     cholesky_panels(aug, 0, panels // 2)
-    for dx in range(1, nx):
-        ag1x(dx).wait_recv()
-    for dy in range(1, ny):
-        ag2x(dy).start()
-    for dy in range(1, ny):
-        ag1y(dy).wait_recv()
-    for dx in range(1, nx):
-        ag2y(dx).start()
+    right_out.second()
     cholesky_panels(aug, panels // 2, panels)
     inverse = aug[:, k:]
     inv_out[...] = inverse
     lhat_out[...] = dot32(dot32(left, inverse, ((1,), (1,))), inverse)
-
-    for dy in range(1, ny):
-        ag2x(dy).wait_recv()
-    for dx in range(1, nx):
-        ag2y(dx).wait_recv()
-    share = d2d(0, (slice(None), slice(None), pl.ds(pl.multiple_of(c * hc, hc), hc)))
-    share.start()
-    share.wait_recv()
-    sown_out[...] = s_full[j // ny, j % ny]
+    right_out.third()
+    right_out.last()
+    sown_out[...] = ordered(s_full, j // ny, j % ny)
 
     for wait in pending:
         wait()
-    share.wait_send()
-
-
-def split(v):
-    high = v.astype(jnp.bfloat16)
-    return high, (v - high.astype(F32)).astype(jnp.bfloat16)
+
+
+def ordered(ref, *index):
+    cores, depth = ref.shape[-4], ref.shape[-3]
+    return jnp.concatenate([ref[(*index, c, z)] for z in range(depth) for c in range(cores)], axis=0)
+
+
+def rows_of(ref):
+    return ref.shape[1] * ref.shape[2] * ref.shape[3]
 
 
 def finish_body(wide, merged, lhat, s, momentum, sown, inverse, error, new_momentum, right, e_buf, m_buf, sem):
@@ -541,7 +568,8 @@
 
     for i in range(total // wide):
         cols = pl.ds(i * wide, wide)
-        s_high, s_low = split(s[cols, :])
+        blocks = wide // rows_of(s)
+        s_high, s_low = split(jnp.concatenate([ordered(s, i * blocks + h) for h in range(blocks)], axis=0))
         s_all = jnp.concatenate([s_high, s_low, s_high], axis=1)
         approx = lax.dot_general(l_all, s_all, (((1,), (1,)), ((), ())), preferred_element_type=F32)
         e_buf[i] = merged[:, cols] - approx
@@ -568,7 +596,7 @@
         vmem((nz, 2, tok, cb), jnp.bfloat16),
         vmem((rows, tok), jnp.bfloat16),
         vmem((rows, total), F32),
-        vmem((cb, k), F32),
+        vmem((nx, ny, 2, nz, sr, k), F32),
         vmem((rows, cb), F32),
         vmem((cb, rows), F32),
         vmem((n, hr + SCALE_ROWS, cb), jnp.bfloat16),
@@ -584,22 +612,26 @@
         vmem((2, n, sr, k), F32),
         vmem((2, n - 1, sr, k), F32),
         vmem((2, n, sr, k), F32),
-        vmem((2, n, sr + gr, k), F32),
-        vmem((2, n - 1, sr + gr, k), F32),
-        vmem((2, n, sr + gr, k), F32),
+        vmem((2, n, sr, k), F32),
+        vmem((2, n - 1, sr, k), F32),
+        vmem((2, n, sr, k), F32),
+        vmem((2, n, gr, k), F32),
+        vmem((2, n - 1, gr, k), F32),
+        vmem((2, n, gr, k), F32),
         vmem((k, 2 * k), F32),
         dma((4,)),
-        dma((far, 2)), dma((far, 2)), dma((far, 2)), dma((far, 2)),
-        dma((nz, 2)), dma((nz, 2)),
-        dma((3,)), dma,
+        dma((far, PARTS)), dma((far, PARTS)), dma((far, PARTS)), dma((far, PARTS)),
+        dma((nz, PARTS)), dma((nz, PARTS)),
+        dma((2,)), dma((2,)),
         dma((n,)), dma((ny, max(nx - 1, 1))),
         dma((n,)), dma((nx, max(ny - 1, 1))),
         dma((max(ny - 1, 1),)), dma((max(ny - 1, 1),)),
         dma((max(nx - 1, 1),)), dma((max(nx - 1, 1),)),
         dma((2,)), dma((2,)), dma((2,)), dma((2,)),
         dma((2,)), dma((2,)), dma((2,)), dma((2,)),
-        dma((4, max(nx, ny))), dma((4, max(nx, ny))),
-        dma((1,)), dma((1,)),
+        dma((2,)), dma((2,)), dma((2,)), dma((2,)),
+        dma((2, 4, max(nx, ny))), dma((2, 4, max(nx, ny))),
+        dma((2, nx + ny)), dma((2, nx + ny)),
     ]
     any_space = pl.BlockSpec(memory_space=pl.ANY)
     in_vmem = pl.BlockSpec(memory_space=pltpu.VMEM)
@@ -608,7 +640,7 @@
         out_shape=(
             jax.ShapeDtypeStruct((rows, total), F32),
             jax.ShapeDtypeStruct((rows, k), F32),
-            jax.ShapeDtypeStruct((nx, ny, cb, k), F32),
+            jax.ShapeDtypeStruct((nx, ny, 2, nz, sr, k), F32),
             jax.ShapeDtypeStruct((cb, k), F32),
             jax.ShapeDtypeStruct((k, k), F32),
             jax.ShapeDtypeStruct((rows, total), momentum.dtype),
@@ -621,7 +653,7 @@
         ),
         name="compress",
     )(*[pltpu.with_memory_space_constraint(v, pltpu.HBM) for v in (grad_out, activations, error_feedback, right_factor, momentum)])
-    s = s.reshape(n * cb, k)
+    s = s.reshape(n, 2, nz, sr, k)
     wide = min(512, total)
     return pl.pallas_call(
         functools.partial(finish_body, wide),

time: 119 us -> 115 us (0.966)
  Pallas kernels: 118 us -> 114 us
    pallas_call x1, Pallas kernels: 114 us -> 111 us  [per_device(): pl.pallas_call(functools.partial(body, nx, ny, nz, 1.0 / n), out_shape=(j...]
where the time goes in v3:
time: 115 us
  Pallas kernels  114 us (99%)
    pallas_call x1, Pallas kernels, per_device(): pl.pallas_call(functools.partial(body, nx, ny, nz, 1.0 / n), out_shape=(j...  111 us
    pallas_call x1, Pallas kernels, per_device(): pl.pallas_call(functools.partial(finish_body, wide), out_shape=(jax.Shape...  3.84 us

profile of v3, /device:TPU:1, one launch (start us, length us, event | category | flops | bytes accessed | tf_op | source)
XLA Modules:
  0.0 115.3 jit_solution(16086600955569265184)
XLA Ops:
  0.6 110.6 %compress.1 = (f32[256,4096]{1,0:T(8,128)S(1)}, f32[256,128]{1,0:T(8,128)S(1)}, f32[4,4,2,8,16,128]{5,4,3,2,1,0:T(8,128)S(1)}, f32[256,128]{1,0:T(8,128)S(1)}, f...) custom-call(bf16[512,256]{1,0:T(8,128)(2,1)} %grad.1, bf16[512,256]{1,0:T(8,128)(2,1)} %act.1, f32[1,256,4096]{2,1,0:T(8,128)} %err.1, ...), custom_call_target="tpu_custom_call" | custom-call | tf_op jit(solution)/shard_map/compress/pallas_call | solution.py:638
  111.3 3.8 %finish.1 = (f32[1,256,4096]{2,1,0:T(8,128)}, bf16[256,4096]{1,0:T(8,128)(2,1)}, f32[256,128]{1,0:T(8,128)}) custom-call(f32[256,4096]{1,0:T(8,128)S(1)} %get-tuple-element.9.merged, f32[256,128]{1,0:T(8,128)S(1)} %get-tuple-element.10.lhat, f32[16,2,8,16,128]{4,3,2,1,0:T(8,128)S(1)} %bitcast.1, bf16[256,4096]{1,0:T(8,128)(2,1)S(1)} %get-tuple-element.12.momentum, ...), custom_call_target="tpu_custom_call" | custom-call | tf_op jit(solution)/shard_map/finish/pallas_call | solution.py:658

commit v4 on v3

--- a/solution.py
+++ b/solution.py
@@ -13,7 +13,6 @@
 F32 = jnp.float32
 PANEL = 16
 SCALE_ROWS = 16
-LAG = 5
 PARTS = 4
 VMEM_LIMIT = 33_554_432
 
@@ -60,11 +59,9 @@
 def dot_split(a, b):
     a_high, a_low = split(a)
     b_high, b_low = split(b)
-    return jnp.dot(
-        jnp.concatenate([a_high, a_high, a_low], axis=1),
-        jnp.concatenate([b_high, b_low, b_high], axis=0),
-        preferred_element_type=F32,
-    )
+    k = b.shape[1]
+    wide = jnp.dot(a_high, jnp.concatenate([b_high, b_low], axis=1), preferred_element_type=F32)
+    return wide[:, :k] + (wide[:, k:] + jnp.dot(a_low, b_high, preferred_element_type=F32))
 
 
 def cholesky_panels(aug, first, last):
@@ -297,24 +294,25 @@
         return decode(message[:half_rows], message[half_rows:])
 
     def produce(slot, dc):
-        if dc == 1:
-            for h in range(PARTS):
-                sibling(slot, h).wait_recv()
+        cols = columns(block_of(slot, dc))
+        merged[:, cols] = jnp.dot(grad_t[...], act_all[slot, dc], preferred_element_type=F32) + err_v[:, cols]
+
+    def send(slot, dc):
         b = block_of(slot, dc)
-        cols = columns(b)
-        tile = jnp.dot(grad_t[...], act_all[slot, dc], preferred_element_type=F32) + err_v[:, cols]
-        merged[:, cols] = tile
         owner_x, owner_y = b // ny, b % ny
         at = 2 * slot + dc
+        code, peak = encode(merged[:, columns(b)])
+        xt[at, :half_rows] = code[:half_rows]
+        yt[at, :half_rows] = code[half_rows:]
+        xt[at, half_rows:] = peak
+        yt[at, half_rows:] = peak
         if nx > 1:
             @pl.when(owner_x != x)
             def _():
-                put(xt, at, tile[:half_rows])
                 x_copy(b, (owner_x - x + nx) % nx, at).start()
         if ny > 1:
             @pl.when(owner_y != y)
             def _():
-                put(yt, at, tile[half_rows:])
                 y_copy(b, (owner_y - y + ny) % ny, at).start()
 
     def xf_copy(dy):
@@ -363,29 +361,32 @@
                 yf_copy(dx).start()
 
     def tiles_sent():
-        for slot in range(nz):
-            for dc in (0, 1):
-                b, at = block_of(slot, dc), 2 * slot + dc
-
-                @pl.when(b // ny != x)
-                def _(b=b, at=at):
-                    x_copy(b, 1, at).wait_send()
-
-                @pl.when(b % ny != y)
-                def _(b=b, at=at):
-                    y_copy(b, 1, at).wait_send()
+        @pl.loop(0, n)
+        def _(at):
+            b = block_of(at // 2, at % 2)
+
+            @pl.when(b // ny != x)
+            def _():
+                x_copy(b, 1, at).wait_send()
+
+            @pl.when(b % ny != y)
+            def _():
+                y_copy(b, 1, at).wait_send()
         for dy in range(1, ny):
             xf_copy(dy).wait_send()
         for dx in range(1, nx):
             yf_copy(dx).wait_send()
 
-    def multiply(pairs):
-        total = jnp.zeros((rb_rows, k), F32)
-        for slot, dc in pairs:
-            b = block_of(slot, dc)
-            strips = [r_all[i, h, b % 2, b // 2] for h in range(ny) for i in range(nx)]
-            total = total + dot_split(merged[:, columns(b)], jnp.concatenate(strips, axis=0))
-        return total
+    def multiply(slot, dc):
+        b = block_of(slot, dc)
+        strips = [r_all[i, h, b % 2, b // 2] for h in range(ny) for i in range(nx)]
+        product = dot_split(merged[:, columns(b)], jnp.concatenate(strips, axis=0))
+        p_plane[0] = p_plane[0] + (product * scale).reshape(n, sr, k)
+
+    def ring_pair(s, act):
+        @pl.loop(0, jnp.where(s == 0, 1, 2))
+        def _(t):
+            act(jnp.where(t == 0, (nz - s) % nz, s))
 
     def plane_scatter(stage):
         pending.append(lambda: wait_bytes(r_plane.at[stage], ps_send.at[stage]))
@@ -408,50 +409,109 @@
         return f_plane[stage].reshape(rb_rows, k)
 
     pending.append(tiles_sent)
+    p_plane[0] = jnp.zeros((n, sr, k), F32)
+    steps = len(up_list)
+    gathered_late = steps <= 12
     produce(0, 0)
-    later = [[] for _ in range(len(up_list) + 1)]
-    later[0].append((0, 1))
-    for i, (s, h) in enumerate(up_list):
-        if s < far and h == PARTS - 1:
-            later[i] += [(nz - s, 0), (s, 0)]
-            later[i + 1] += [(nz - s, 1), (s, 1)]
-    later[len(up_list) - 1] += [(far, 0), (far, 1)]
-    waiting = [[(0, 0)]]
-    steps = len(up_list)
-    multiplied = []
-    for i, ((s, h), (t, g)) in enumerate(zip(up_list, down_list)):
+    send(0, 0)
+
+    def ring_step(i):
+        s, h = i // PARTS + 1, i % PARTS
+        more = jnp.logical_or(s + 1 < far, jnp.logical_and(s + 1 == far, h < mid))
         up(s, h).wait_recv()
-        if s + 1 < far or (s + 1 == far and h < mid):
+
+        @pl.when(more)
+        def _():
             up(s + 1, h).start()
         sibling(nz - s, h).start()
-        down(t, g).wait_recv()
-        if t + 1 < far or (t + 1 == far and g >= mid):
-            down(t + 1, g).start()
-        sibling(t, g).start()
-        if i == min(2, steps - 1):
-            right_in.column_wait()
-            right_in.first()
-        if i == min(6, steps - 1):
-            right_in.second()
-        if i == min(11, steps - 1):
-            right_in.third()
-        for slot, dc in later[i]:
-            produce(slot, dc)
-        waiting.append(later[i])
-        if len(waiting) > LAG:
-            for slot, dc in waiting.pop(0):
-                consume(slot, dc)
-        if i == max(steps - 2, min(11, steps - 1)):
-            right_in.last()
-            multiplied = [(0, 0)] + [pair for group in later[: i + 1] for pair in group]
-            left_sum = multiply(multiplied)
-    rest = [pair for group in later for pair in group if pair not in multiplied]
-    p_plane[0] = ((left_sum + multiply(rest)) * scale).reshape(n, sr, k)
+        down(s, PARTS - 1 - h).wait_recv()
+
+        @pl.when(more)
+        def _():
+            down(s + 1, PARTS - 1 - h).start()
+        sibling(s, PARTS - 1 - h).start()
+
+    @pl.loop(0, steps - 1)
+    def _(i):
+        ring_step(i)
+        if not gathered_late:
+            @pl.when(i == 1)
+            def _():
+                right_in.column_wait()
+                right_in.first()
+
+            @pl.when(i == 5)
+            def _():
+                right_in.second()
+
+            @pl.when(i == 9)
+            def _():
+                right_in.third()
+
+            @pl.when(i == 10)
+            def _():
+                right_in.last()
+
+                @pl.loop(0, 2 * (far - 1))
+                def _(t):
+                    ring_pair(t // 2, lambda slot: multiply(slot, t % 2))
+
+        @pl.when(jnp.logical_or(i % PARTS == PARTS - 1, i % PARTS == 0))
+        def _():
+            s, dc = (i + 1) // PARTS, jnp.where(i % PARTS == 0, 1, 0)
+
+            @pl.when(dc == 1)
+            def _():
+                def landed(slot):
+                    for h in range(PARTS):
+                        sibling(slot, h).wait_recv()
+                ring_pair(s, landed)
+
+            def fresh(slot):
+                produce(slot, dc)
+                send(slot, dc)
+            ring_pair(s, fresh)
+
+            @pl.when(s > 0)
+            def _():
+                ring_pair(s - 1, lambda slot: consume(slot, dc))
+
+    ring_step(steps - 1)
+    if gathered_late:
+        right_in.column_wait()
+        right_in.first()
+        right_in.second()
+        right_in.third()
+        right_in.last()
+
+        @pl.loop(0, 2 * (far - 1))
+        def _(t):
+            ring_pair(t // 2, lambda slot: multiply(slot, t % 2))
+
+    @pl.loop(0, 2)
+    def _(dc):
+        ring_pair(far - 1, lambda slot: multiply(slot, dc))
+    for h in range(PARTS):
+        sibling(far, h).wait_recv()
+
+    @pl.loop(0, 2)
+    def _(dc):
+        produce(far, dc)
+        multiply(far, dc)
     plane_scatter(0)
-    for group in waiting:
-        for slot, dc in group:
-            consume(slot, dc)
+
+    @pl.loop(0, 2)
+    def _(dc):
+        send(far, dc)
+
+    @pl.loop(0, 2)
+    def _(dc):
+        ring_pair(far - 1, lambda slot: consume(slot, dc))
     plane_gather(0)
+
+    @pl.loop(0, 2)
+    def _(dc):
+        consume(far, dc)
 
     acc = top[...]
     for dy in range(1, ny):
@@ -496,7 +556,7 @@
         return full[stage].reshape(-1, k)
 
     def right_of(stage, left):
-        p_col[stage] = dot32(m_t[...], left).reshape(n, sr, k)
+        p_col[stage] = dot_split(m_t[...], left).reshape(n, sr, k)
         col_scatter(stage, factor_col, stage == 0)
         p_gram[stage] = dot32(left, left, ((0,), (0,))).reshape(n, gr, k)
         col_scatter(stage, gram_col)
@@ -519,7 +579,7 @@
     left = plane_finish(0)
     right_of(0, left)
     s_one = col_finish(0, factor_col)
-    p_plane[1] = dot32(m_tile[...], s_one).reshape(n, sr, k)
+    p_plane[1] = dot_split(m_tile[...], s_one).reshape(n, sr, k)
     plane_scatter(1)
     set_aug(col_finish(0, gram_col))
     cholesky_panels(aug, 0, panels // 2)

time: 115 us -> 117 us (1.017)
  Pallas kernels: 114 us -> 116 us
    pallas_call x1, Pallas kernels: 111 us -> 112 us  [per_device(): pl.pallas_call(functools.partial(body, nx, ny, nz, 1.0 / n), out_shape=(j...]
where the time goes in v4:
time: 117 us
  Pallas kernels  116 us (99%)
    pallas_call x1, Pallas kernels, per_device(): pl.pallas_call(functools.partial(body, nx, ny, nz, 1.0 / n), out_shape=(j...  112 us
    pallas_call x1, Pallas kernels, per_device(): pl.pallas_call(functools.partial(finish_body, wide), out_shape=(jax.Shape...  3.84 us

profile of v4, /device:TPU:1, one launch (start us, length us, event | category | flops | bytes accessed | tf_op | source)
XLA Modules:
  0.0 116.8 jit_solution(9350699083308043498)
XLA Ops:
  0.6 112.3 %compress.1 = (f32[256,4096]{1,0:T(8,128)S(1)}, f32[256,128]{1,0:T(8,128)S(1)}, f32[4,4,2,8,16,128]{5,4,3,2,1,0:T(8,128)S(1)}, f32[256,128]{1,0:T(8,128)S(1)}, f...) custom-call(bf16[512,256]{1,0:T(8,128)(2,1)} %grad.1, bf16[512,256]{1,0:T(8,128)(2,1)} %act.1, f32[1,256,4096]{2,1,0:T(8,128)} %err.1, ...), custom_call_target="tpu_custom_call" | custom-call | tf_op jit(solution)/shard_map/compress/pallas_call | solution.py:698
  113.0 3.8 %finish.1 = (f32[1,256,4096]{2,1,0:T(8,128)}, bf16[256,4096]{1,0:T(8,128)(2,1)}, f32[256,128]{1,0:T(8,128)}) custom-call(f32[256,4096]{1,0:T(8,128)S(1)} %get-tuple-element.9.merged, f32[256,128]{1,0:T(8,128)S(1)} %get-tuple-element.10.lhat, f32[16,2,8,16,128]{4,3,2,1,0:T(8,128)S(1)} %bitcast.1, bf16[256,4096]{1,0:T(8,128)(2,1)S(1)} %get-tuple-element.12.momentum, ...), custom_call_target="tpu_custom_call" | custom-call | tf_op jit(solution)/shard_map/finish/pallas_call | solution.py:718

commit v5 on v3

--- a/solution.py
+++ b/solution.py
@@ -60,11 +60,9 @@
 def dot_split(a, b):
     a_high, a_low = split(a)
     b_high, b_low = split(b)
-    return jnp.dot(
-        jnp.concatenate([a_high, a_high, a_low], axis=1),
-        jnp.concatenate([b_high, b_low, b_high], axis=0),
-        preferred_element_type=F32,
-    )
+    k = b.shape[1]
+    wide = jnp.dot(a_high, jnp.concatenate([b_high, b_low], axis=1), preferred_element_type=F32)
+    return wide[:, :k] + (wide[:, k:] + jnp.dot(a_low, b_high, preferred_element_type=F32))
 
 
 def cholesky_panels(aug, first, last):
@@ -300,21 +298,25 @@
         if dc == 1:
             for h in range(PARTS):
                 sibling(slot, h).wait_recv()
+        cols = columns(block_of(slot, dc))
+        merged[:, cols] = jnp.dot(grad_t[...], act_all[slot, dc], preferred_element_type=F32) + err_v[:, cols]
+
+    def send(slot, dc):
         b = block_of(slot, dc)
-        cols = columns(b)
-        tile = jnp.dot(grad_t[...], act_all[slot, dc], preferred_element_type=F32) + err_v[:, cols]
-        merged[:, cols] = tile
         owner_x, owner_y = b // ny, b % ny
         at = 2 * slot + dc
+        code, peak = encode(merged[:, columns(b)])
+        xt[at, :half_rows] = code[:half_rows]
+        yt[at, :half_rows] = code[half_rows:]
+        xt[at, half_rows:] = peak
+        yt[at, half_rows:] = peak
         if nx > 1:
             @pl.when(owner_x != x)
             def _():
-                put(xt, at, tile[:half_rows])
                 x_copy(b, (owner_x - x + nx) % nx, at).start()
         if ny > 1:
             @pl.when(owner_y != y)
             def _():
-                put(yt, at, tile[half_rows:])
                 y_copy(b, (owner_y - y + ny) % ny, at).start()
 
     def xf_copy(dy):
@@ -409,6 +411,7 @@
 
     pending.append(tiles_sent)
     produce(0, 0)
+    send(0, 0)
     later = [[] for _ in range(len(up_list) + 1)]
     later[0].append((0, 1))
     for i, (s, h) in enumerate(up_list):
@@ -431,27 +434,34 @@
         if i == min(2, steps - 1):
             right_in.column_wait()
             right_in.first()
-        if i == min(6, steps - 1):
+        if i == min(5, steps - 1):
             right_in.second()
-        if i == min(11, steps - 1):
+        if i == min(10, steps - 1):
             right_in.third()
         for slot, dc in later[i]:
             produce(slot, dc)
+        if i < steps - 1:
+            for slot, dc in later[i]:
+                send(slot, dc)
         waiting.append(later[i])
-        if len(waiting) > LAG:
+        if i < steps - 1 and len(waiting) > LAG:
             for slot, dc in waiting.pop(0):
                 consume(slot, dc)
-        if i == max(steps - 2, min(11, steps - 1)):
+        if i == max(steps - 3, min(10, steps - 1)):
             right_in.last()
             multiplied = [(0, 0)] + [pair for group in later[: i + 1] for pair in group]
             left_sum = multiply(multiplied)
     rest = [pair for group in later for pair in group if pair not in multiplied]
     p_plane[0] = ((left_sum + multiply(rest)) * scale).reshape(n, sr, k)
     plane_scatter(0)
-    for group in waiting:
+    for slot, dc in later[steps - 1]:
+        send(slot, dc)
+    for group in waiting[:-1]:
         for slot, dc in group:
             consume(slot, dc)
     plane_gather(0)
+    for slot, dc in waiting[-1]:
+        consume(slot, dc)
 
     acc = top[...]
     for dy in range(1, ny):
@@ -496,7 +506,7 @@
         return full[stage].reshape(-1, k)
 
     def right_of(stage, left):
-        p_col[stage] = dot32(m_t[...], left).reshape(n, sr, k)
+        p_col[stage] = dot_split(m_t[...], left).reshape(n, sr, k)
         col_scatter(stage, factor_col, stage == 0)
         p_gram[stage] = dot32(left, left, ((0,), (0,))).reshape(n, gr, k)
         col_scatter(stage, gram_col)
@@ -519,7 +529,7 @@
     left = plane_finish(0)
     right_of(0, left)
     s_one = col_finish(0, factor_col)
-    p_plane[1] = dot32(m_tile[...], s_one).reshape(n, sr, k)
+    p_plane[1] = dot_split(m_tile[...], s_one).reshape(n, sr, k)
     plane_scatter(1)
     set_aug(col_finish(0, gram_col))
     cholesky_panels(aug, 0, panels // 2)

time: 115 us -> 113 us (0.983)
  Pallas kernels: 114 us -> 112 us
    pallas_call x1, Pallas kernels: 111 us -> 108 us  [per_device(): pl.pallas_call(functools.partial(body, nx, ny, nz, 1.0 / n), out_shape=(j...]
where the time goes in v5:
time: 113 us
  Pallas kernels  112 us (99%)
    pallas_call x1, Pallas kernels, per_device(): pl.pallas_call(functools.partial(body, nx, ny, nz, 1.0 / n), out_shape=(j...  108 us
    pallas_call x1, Pallas kernels, per_device(): pl.pallas_call(functools.partial(finish_body, wide), out_shape=(jax.Shape...  3.84 us

profile of v5, /device:TPU:1, one launch (start us, length us, event | category | flops | bytes accessed | tf_op | source)
XLA Modules:
  0.0 112.8 jit_solution(1651239104759682148)
XLA Ops:
  0.6 108.2 %compress.1 = (f32[256,4096]{1,0:T(8,128)S(1)}, f32[256,128]{1,0:T(8,128)S(1)}, f32[4,4,2,8,16,128]{5,4,3,2,1,0:T(8,128)S(1)}, f32[256,128]{1,0:T(8,128)S(1)}, f...) custom-call(bf16[512,256]{1,0:T(8,128)(2,1)} %grad.1, bf16[512,256]{1,0:T(8,128)(2,1)} %act.1, f32[1,256,4096]{2,1,0:T(8,128)} %err.1, ...), custom_call_target="tpu_custom_call" | custom-call | tf_op jit(solution)/shard_map/compress/pallas_call | solution.py:648
  108.8 3.8 %finish.1 = (f32[1,256,4096]{2,1,0:T(8,128)}, bf16[256,4096]{1,0:T(8,128)(2,1)}, f32[256,128]{1,0:T(8,128)}) custom-call(f32[256,4096]{1,0:T(8,128)S(1)} %get-tuple-element.9.merged, f32[256,128]{1,0:T(8,128)S(1)} %get-tuple-element.10.lhat, f32[16,2,8,16,128]{4,3,2,1,0:T(8,128)S(1)} %bitcast.1, bf16[256,4096]{1,0:T(8,128)(2,1)S(1)} %get-tuple-element.12.momentum, ...), custom_call_target="tpu_custom_call" | custom-call | tf_op jit(solution)/shard_map/finish/pallas_call | solution.py:668
